TPU v7x, 128 devices: a whole 4x4x4 slice. The times are simulated.
128 devices in a mesh: layer: 8 (over z_lo, y), lat: 16 (over x, z_hi, core).
Axes of the slice: x: 4, y: 4, z: 4 (z_hi: 2, z_lo: 2; z = z_hi * 2 + z_lo), core: 2. Of those that a mesh axis runs over, the one named last changes fastest.
Arguments:
- activations: bfloat16 [8, 512, 2048], P(None, None, 'layer'), may hold values from -6 to 6
- targets: bfloat16 [8, 512, 2048], P(None, None, 'layer'), may hold values from -6 to 6
- encoder: bfloat16 [8, 2048, 8192], P(None, 'layer', 'lat'), may hold values from -0.125 to 0.125
- bias: float32 [8, 8192], P(None, 'lat'), may hold values from -3 to 3
- decoder: bfloat16 [36, 8192, 2048], P(None, 'lat', 'layer'), may hold values from -0.75 to 0.75
- active: int32 [8, 512, 64], replicated, may hold values from 0 to 8191, all different within a row
Outputs:
- grad_encoder: bfloat16 [8, 2048, 8192], P(None, 'layer', 'lat')
- grad_bias: float32 [8, 8192], P(None, 'lat')
- grad_decoder: bfloat16 [36, 8192, 2048], P(None, 'lat', 'layer')
Inputs may be any that keep to these rules, and one draw needn't show every extreme that they name: `active`: each row names 64 different latents.
All inputs are finite; a program needn't handle non-finite values.
Results may differ from a plain program's by a relative error of at most 0.0064.
Values may be sent and summed in bfloat16 or wider, within the bound.
No kernel may reach another device: no remote copies, remote signals or barrier semaphores. Data moves between devices by JAX's collectives and lax.ppermute only.
A program may use at most 128 MiB of HBM per device.

v0:
```python
import jax
import jax.numpy as jnp
from jax import lax
from jax.sharding import PartitionSpec as P

LAYERS = 8


def padded_to(lines, size):
    spare = -len(lines) % size
    return jnp.pad(lines, [(0, spare)] + [(0, 0)] * (lines.ndim - 1))


def sum_by_parts(x, axis):
    lines = x.reshape(-1, *x.shape[1:][-1:])
    own = lax.psum_scatter(
        padded_to(lines, lax.axis_size(axis)), axis, scatter_dimension=0, tiled=True
    )
    whole = lax.all_gather(own, axis).reshape(-1, *lines.shape[1:])
    return lax.slice_in_dim(whole, 0, len(lines)).reshape(x.shape)


def pair_index(source, target):
    return source * LAYERS - source * (source - 1) // 2 + (target - source)


def on_device(activations, targets, encoder, bias, decoder, active):
    lat_width = encoder.shape[2]
    first = lax.axis_index("lat") * lat_width
    columns = first + jnp.arange(lat_width, dtype=jnp.int32)
    masks = jnp.stack(
        [
            jnp.any(active[source][:, :, None] == columns[None, None, :], axis=1)
            for source in range(LAYERS)
        ]
    ).astype(jnp.float32)
    partial_value = jnp.einsum(
        "ltd,ldf->ltf", activations, encoder, preferred_element_type=jnp.float32
    )
    preact = lax.psum(partial_value, "layer") + bias[:, None, :]
    latent_act = (preact * masks).astype(jnp.bfloat16)
    rebuilt_list = []
    for target in range(LAYERS):
        summed = jnp.dot(
            latent_act[0], decoder[pair_index(0, target)], preferred_element_type=jnp.float32
        )
        for source in range(1, target + 1):
            summed = summed + jnp.dot(
                latent_act[source],
                decoder[pair_index(source, target)],
                preferred_element_type=jnp.float32,
            )
        rebuilt_list.append(summed)
    rebuilt = jnp.stack(rebuilt_list)
    complete = lax.psum(rebuilt, "lat")
    errors = (complete - targets.astype(jnp.float32)).astype(jnp.bfloat16)
    by_tokens = (((0,), (0,)), ((), ()))
    by_width = (((1,), (1,)), ((), ()))
    grad_pairs = []
    for source in range(LAYERS):
        for target in range(source, LAYERS):
            grad_pairs.append(
                lax.dot_general(
                    latent_act[source],
                    errors[target],
                    by_tokens,
                    preferred_element_type=jnp.float32,
                ).astype(jnp.bfloat16)
            )
    grad_decoder = jnp.stack(grad_pairs)
    grad_list = []
    for source in range(LAYERS):
        summed = lax.dot_general(
            errors[source],
            decoder[pair_index(source, source)],
            by_width,
            preferred_element_type=jnp.float32,
        )
        for target in range(source + 1, LAYERS):
            summed = summed + lax.dot_general(
                errors[target],
                decoder[pair_index(source, target)],
                by_width,
                preferred_element_type=jnp.float32,
            )
        grad_list.append(summed)
    grad_partial = jnp.stack(grad_list)
    grad_act = sum_by_parts(grad_partial, "layer")
    grad_pre = (grad_act * masks).astype(jnp.bfloat16)
    grad_encoder = jnp.einsum(
        "ltd,ltf->ldf", activations, grad_pre, preferred_element_type=jnp.float32
    ).astype(jnp.bfloat16)
    grad_bias = jnp.sum(grad_pre.astype(jnp.float32), axis=1)
    return (grad_encoder, grad_bias, grad_decoder)


def solution(mesh):
    placed = (
        P(None, None, "layer"),
        P(None, None, "layer"),
        P(None, "layer", "lat"),
        P(None, "lat"),
        P(None, "lat", "layer"),
        P(),
    )
    return jax.shard_map(
        on_device,
        mesh=mesh,
        in_specs=placed,
        out_specs=(P(None, "layer", "lat"), P(None, "lat"), P(None, "lat", "layer")),
        check_vma=False,
    )
```

profile of v0, /device:TPU:1, one launch (start us, length us, event | category | flops | bytes accessed | tf_op | source)
XLA Modules:
  0.0 620.8 jit_solution(13394112168313899540)
XLA Ops:
  7.2 1.5 copy-done
  8.8 6.2 %fusion.261 = f32[8,512,512]{2,1,0:T(8,128)} fusion(bf16[8,512,256]{2,1,0:T(8,128)(2,1)S(1)} %copy-done, bf16[8,256,512]{2,1,0:T(8,128)(2,1)} %param.8), kind=kOutput, calls=%fused_computation.401 | convolution fusion | flops 1073741824 | bytes 12582912 | tf_op jit(solution)/shard_map/ltd,ldf->ltf/dot_general | solution.py:37
  15.1 1.1 copy-done.6
  18.3 1.7 copy.21
  20.0 1.8 copy.22
  21.8 1.7 copy.23
  23.5 1.8 copy.24
  25.3 1.7 copy.25
  27.9 141.5 %compare_reduce_fusion = (pred[512,512]{1,0:T(8,128)(4,1)S(1)}, pred[512,512]{1,0:T(8,128)(4,1)}, pred[512,512]{1,0:T(8,128)(4,1)}, pred[512,512]{1,0:T(8,128)(4...) fusion(s32[512,64]{1,0:T(8,128)S(1)} %copy.26, ...), kind=kLoop, calls=%fused_computation | loop fusion | flops 266338304 | bytes 3147776 | tf_op jit(solution)/shard_map/reduce_or | solution.py:33
  169.4 1.7 bitcast_dynamic-update-slice_fusion.7
  171.1 1.7 bitcast_dynamic-update-slice_fusion.6
  172.8 1.7 bitcast_dynamic-update-slice_fusion.5
  174.5 1.7 bitcast_dynamic-update-slice_fusion.4
  176.2 1.7 bitcast_dynamic-update-slice_fusion.3
  180.0 22.6 %all-reduce.3.cloned.1.call-done = f32[8,512,512]{2,1,0:T(8,128)} async-done(((f32[8,512,512]{2,1,0:T(8,128)}), f32[8,512,512]{2,1,0:T(8,128)}) %all-reduce.3.cloned.1.call-update) | async-done | bytes 8388624 | tf_op jit(solution)/shard_map/psum | solution.py:40
  202.6 5.9 select_convert_fusion.1
  208.5 2.3 fusion.15
  210.9 1.2 fusion.183
  212.1 1.2 fusion.177
  213.4 1.2 fusion.169
  214.6 1.2 fusion.159
  215.9 1.2 fusion.147
  224.1 1.1 fusion.29
  225.2 1.1 fusion.27
  226.3 1.1 fusion.25
  227.4 1.1 fusion.23
  228.5 1.1 fusion.21
  229.6 1.1 fusion.19
  230.7 1.1 fusion.17
  232.1 150.5 %all-reduce.5.cloned.1.call-done = f32[8,512,256]{2,1,0:T(8,128)} async-done(((f32[8,512,256]{2,1,0:T(8,128)}), f32[8,512,256]{2,1,0:T(8,128)}) %all-reduce.5.cloned.1.call-update) | async-done | bytes 4194320 | tf_op jit(solution)/shard_map/psum | solution.py:55
  382.6 3.5 subtract_convert_fusion
  386.1 2.8 fusion.185
  388.9 1.3 fusion.179
  390.2 1.4 fusion.171
  391.6 1.3 fusion.161
  392.8 1.3 fusion.149
  394.1 1.3 fusion.135
  395.4 1.3 fusion.119
  406.5 3.4 copy-done.5
  410.2 94.0 %reduce-scatter.2.cloned.1.call-done = f32[512,512]{1,0:T(8,128)} async-done(((f32[4096,512]{1,0:T(8,128)}), f32[512,512]{1,0:T(8,128)}) %reduce-scatter.2.cloned.1.call-update) | async-done | bytes 1048592 | tf_op jit(solution)/shard_map/reduce_scatter | solution.py:16
  504.3 2.3 fusion.31
  506.6 2.2 fusion.33
  508.8 2.2 fusion.35
  510.9 2.0 fusion.37
  512.9 1.1 fusion.39
  514.0 1.1 fusion.41
  515.0 1.1 fusion.43
  519.2 1.1 fusion.51
  520.3 1.1 fusion.53
  521.3 1.1 fusion.55
  525.5 1.1 fusion.63
  526.6 1.1 fusion.65
  527.6 1.1 fusion.67
  531.8 1.1 fusion.75
  532.9 1.1 fusion.77
  533.9 1.1 fusion.79
  538.1 1.1 fusion.87
  539.2 1.1 fusion.89
  540.3 1.1 fusion.91
  545.5 1.1 fusion.101
  546.6 49.8 %all-gather.3.cloned.1.call-done = f32[4096,512]{1,0:T(8,128)} async-done(((f32[512,512]{1,0:T(8,128)}), f32[4096,512]{1,0:T(8,128)}) %all-gather.3.cloned.1.call-update) | async-done | bytes 8388624 | tf_op jit(solution)/shard_map/all_gather | solution.py:19
  596.3 7.5 %convert_bitcast_fusion = bf16[8,256,512]{1,2,0:T(8,128)(2,1)} fusion(bf16[8,512,256]{2,1,0:T(8,128)(2,1)S(1)} %copy-done, pred[8,512,512]{2,1,0:T(8,128)(4,1)} %bitcast_dynamic-update-slice_fusion, f32[8,512,512]{2,1,0:T(8,128)} %bitcast.608), kind=kOutput, calls=%fused_computation.12 | convolution fusion | flops 1076887552 | bytes 14680064 | tf_op jit(solution)/shard_map/ltd,ltf->ldf/dot_general | solution.py:90
  603.8 3.9 copy.28
  607.8 6.0 convert_reduce_fusion
  (111 shorter events, 38.9 us)
Async XLA Ops:
  7.2 1.6 copy-start
  7.2 195.4 %all-reduce.3.cloned.1.call-start = ((), (), s32[]{:S(2)}) async-start(), calls=%async_computation.1 | async-start | bytes 16777216 | tf_op jit(solution)/shard_map/psum | solution.py:40
  15.0 1.2 copy-start.6
  15.0 367.5 %all-reduce.5.cloned.1.call-start = ((), (), s32[]{:S(2)}) async-start(), calls=%async_computation.2 | async-start | bytes 8388608 | tf_op jit(solution)/shard_map/psum | solution.py:55
  27.9 174.7 %copy-start.7 = (f32[8,512]{1,0:T(8,128)S(1)}, f32[8,512]{1,0:T(8,128)}, u32[]{:S(2)}) copy-start(f32[8,512]{1,0:T(8,128)} %param.9) | copy-start | bytes 49156
  202.6 14.6 %slice-start = ((s8[9437184]{0:T(1024)(128)(4,1)}), s8[4194304]{0:T(1024)(128)(4,1)S(1)}, s32[]{:S(2)}) async-start(s8[9437184]{0:T(1024)(128)(4,1)} %bitcast.604), calls=%async_computation.5 | async-start | bytes 8388608
  202.6 14.6 %slice-start.1 = ((s8[9437184]{0:T(1024)(128)(4,1)}), s8[4194304]{0:T(1024)(128)(4,1)S(1)}, s32[]{:S(2)}) async-start(s8[9437184]{0:T(1024)(128)(4,1)} %bitcast.604), calls=%async_computation.6 | async-start | bytes 8388608
  208.5 22.2 %copy-start.1 = (bf16[8,512,512]{2,1,0:T(8,128)(2,1)}, bf16[8,512,512]{2,1,0:T(8,128)(2,1)S(1)}, u32[]{:S(2)}) copy-start(bf16[8,512,512]{2,1,0:T(8,128)(2,1)S(1)} %select_convert_fusion.1) | copy-start | bytes 12582916
  208.5 8.6 %slice-start.2 = ((s8[9437184]{0:T(1024)(128)(4,1)}), s8[1048576]{0:T(1024)(128)(4,1)S(1)}, s32[]{:S(2)}) async-start(s8[9437184]{0:T(1024)(128)(4,1)} %bitcast.604), calls=%async_computation.7 | async-start | bytes 2097152
  231.8 272.4 %reduce-scatter.2.cloned.1.call-start = ((), (), s32[]{:S(2)}) async-start(), calls=%async_computation.3 | async-start | bytes 9437184 | tf_op jit(solution)/shard_map/reduce_scatter | solution.py:16
  382.6 14.1 %slice-start.3 = ((s8[9437184]{0:T(1024)(128)(4,1)}), s8[4194304]{0:T(1024)(128)(4,1)S(1)}, s32[]{:S(2)}) async-start(s8[9437184]{0:T(1024)(128)(4,1)} %bitcast.606), calls=%async_computation.8 | async-start | bytes 8388608
  382.6 14.1 %slice-start.4 = ((s8[9437184]{0:T(1024)(128)(4,1)}), s8[4194304]{0:T(1024)(128)(4,1)S(1)}, s32[]{:S(2)}) async-start(s8[9437184]{0:T(1024)(128)(4,1)} %bitcast.606), calls=%async_computation.9 | async-start | bytes 8388608
  386.1 20.1 %copy-start.3 = (bf16[8,512,256]{2,1,0:T(8,128)(2,1)}, bf16[8,512,256]{2,1,0:T(8,128)(2,1)S(1)}, u32[]{:S(2)}) copy-start(bf16[8,512,256]{2,1,0:T(8,128)(2,1)S(1)} %subtract_convert_fusion) | copy-start | bytes 6291460
  390.2 6.5 %slice-start.5 = ((s8[9437184]{0:T(1024)(128)(4,1)}), s8[1048576]{0:T(1024)(128)(4,1)S(1)}, s32[]{:S(2)}) async-start(s8[9437184]{0:T(1024)(128)(4,1)} %bitcast.606), calls=%async_computation.10 | async-start | bytes 2097152
  406.5 3.4 copy-start.5
  409.9 186.4 %all-gather.3.cloned.1.call-start = ((), (), s32[]{:S(2)}) async-start(), calls=%async_computation.4 | async-start | bytes 9437184 | tf_op jit(solution)/shard_map/all_gather | solution.py:19
  504.3 6.7 %copy-start.2 = (bf16[8,512,512]{2,1,0:T(8,128)(2,1)S(1)}, bf16[8,512,512]{2,1,0:T(8,128)(2,1)}, u32[]{:S(2)}) copy-start(bf16[8,512,512]{2,1,0:T(8,128)(2,1)} %copy-done.1) | copy-start | bytes 12582916
  504.3 8.6 %copy-start.4 = (bf16[8,512,256]{2,1,0:T(8,128)(2,1)S(1)}, bf16[8,512,256]{2,1,0:T(8,128)(2,1)}, u32[]{:S(2)}) copy-start(bf16[8,512,256]{2,1,0:T(8,128)(2,1)} %copy-done.3) | copy-start | bytes 6291460
Sparse Core Ops, SparseCore 0:
  15.2 187.3 all-reduce.2
  231.9 150.5 all-reduce.4
  410.0 94.1 reduce-scatter.1
  505.7 90.5 all-gather.2
where the time goes:
time: 627 us; the launch traced here: 621 us
  waiting for transfers between devices  317 us (51%)
  other arithmetic  157 us (25%)
  matrix products  99 us (16%)
  local copies, waits for them, and re-layouts  32.2 us (5%)
  between operations  15 us (2%)
    psum x1, waiting for transfers between devices, on_device(): complete = lax.psum(rebuilt, 'lat')  150 us
    reduce_or x1, other arithmetic, on_device(): jnp.any(active[source][:, :, None] == columns[None, None, :], axis=1)  142 us
    reduce_scatter x1, waiting for transfers between devices, sum_by_parts(): lax.psum_scatter(padded_to(lines, lax.axis_size(axis)), axis, scatter_dim...  94 us
    all_gather x1, waiting for transfers between devices, sum_by_parts(): whole = lax.all_gather(own, axis).reshape(-1, *lines.shape[1:])  49.8 us
    dot_general x36, matrix products, on_device(): lax.dot_general(latent_act[source], errors[target], by_tokens, preferred_...  42.3 us
    psum x1, waiting for transfers between devices, on_device(): preact = lax.psum(partial_value, 'layer') + bias[:, None, :]  22.6 us
    unnamed x36, local copies, waits for them, and re-layouts  19.8 us
    dot_general x28, matrix products, on_device(): jnp.dot(latent_act[source], decoder[pair_index(source, target)], preferre...  13.8 us
  transfers between devices with their start and end apart: 4, of which 4 were waited for; matrix products, arithmetic and copies ran while one was open for 33% of the time, Pallas kernels for 0%

commit v1 on v0

v1 whole, which is shorter than its diff:
```python
import jax
import jax.numpy as jnp
from jax import lax
from jax.experimental import pallas as pl
from jax.experimental.pallas import tpu as pltpu
from jax.sharding import PartitionSpec as P

LAYERS = 8
T = 512
HALF = T // 2
DW = 256
FW = 512
PAIRS = LAYERS * (LAYERS + 1) // 2
BF = jnp.bfloat16
F32 = jnp.float32
I32 = jnp.int32
BIG = pltpu.CompilerParams(
    dimension_semantics=("arbitrary",), vmem_limit_bytes=60 * 1024 * 1024
)


def first_pair(source):
    return source * LAYERS - source * (source - 1) // 2


def take(x, index):
    return jnp.take_along_axis(x, index, axis=1)


def lanes(rows):
    return lax.broadcasted_iota(I32, (rows, 128), 1)


def slot_columns(table):
    lane = lanes(table.shape[0])
    base = lane & 64
    r = lane & 63
    word_at = jnp.zeros_like(r)
    before = jnp.zeros_like(r)
    for step in (8, 4, 2, 1):
        tried = word_at + step
        count = take(table, base + 16 + tried)
        good = count <= r
        word_at = jnp.where(good, tried, word_at)
        before = jnp.where(good, count, before)
    left = take(table, base + word_at)
    k = r - before
    spot = jnp.zeros_like(r)
    for step in (16, 8, 4, 2, 1):
        low = lax.population_count(left & ((1 << step) - 1))
        good = k >= low
        k = jnp.where(good, k - low, k)
        left = jnp.where(good, lax.shift_right_logical(left, jnp.full_like(left, step)), left)
        spot = jnp.where(good, spot + step, spot)
    return word_at * 32 + spot


def pack(read, columns):
    lane = lanes(HALF)
    within = columns & 127
    chunk_of = lax.shift_right_logical(columns, jnp.full_like(columns, 7))
    packed = None
    for chunk in range(FW // 128):
        picked = jnp.where(
            lane < 64, take(read(0, chunk), within), take(read(1, chunk), within)
        )
        packed = picked if packed is None else jnp.where(chunk_of == chunk, picked, packed)
    return packed


def unpack(table, slots, write):
    lane = lanes(HALF)
    bit = lane & 31
    below = lax.shift_left(jnp.full_like(bit, 1), bit) - 1
    for half in range(2):
        for chunk in range(FW // 128):
            at = 64 * half + 4 * chunk + lax.shift_right_logical(lane, jnp.full_like(lane, 5))
            word = take(table, at)
            before = take(table, at + 16)
            rank = before + lax.population_count(word & below)
            value = take(slots, (rank + 64 * half) & 127)
            hit = (lax.shift_right_logical(word, bit) & 1) == 1
            write(half, chunk, jnp.where(hit, value, 0.0))


def encode_kernel(info, active, acts, encoder, bias, table_out, columns_out, slots_out, rows, dense):
    first = info[0]
    rel = active[0] - first
    high = lax.shift_right_arithmetic(rel, jnp.full_like(rel, 5))
    bits = lax.shift_left(jnp.full_like(rel, 1), rel & 31)
    rows[...] = jnp.zeros_like(rows)
    before = jnp.zeros((1, T), I32)
    for word in range(16):
        marked = jnp.where(high == word, bits, 0)
        folded = marked[0:8]
        for k in range(8, 64, 8):
            folded = folded | marked[k : k + 8]
        whole = jnp.sum(folded, axis=0, keepdims=True)
        for half in range(2):
            part = slice(half * HALF, (half + 1) * HALF)
            rows[64 * half + word : 64 * half + word + 1, :] = whole[:, part]
            rows[64 * half + 16 + word : 64 * half + 17 + word, :] = before[:, part]
        before = before + lax.population_count(whole)
    table = rows[...].T
    table_out[0] = table
    columns = slot_columns(table)
    columns_out[0] = columns
    value = jnp.dot(acts[0], encoder[0], preferred_element_type=F32)
    dense[...] = value + bias[0] * info[1].astype(F32)
    slots_out[0] = pack(
        lambda half, chunk: dense[pl.ds(half * HALF, HALF), pl.ds(chunk * 128, 128)], columns
    ).astype(BF)


def one(*shape):
    return pl.BlockSpec((1,) + shape, lambda i, *_: (i,) + (0,) * len(shape))


def whole(*shape):
    return pl.BlockSpec(shape, lambda i, *_: (0,) * len(shape))


ANY = pl.BlockSpec(memory_space=pl.ANY)


def encode(info, active_t, activations, encoder, bias):
    return pl.pallas_call(
        encode_kernel,
        grid_spec=pltpu.PrefetchScalarGridSpec(
            num_scalar_prefetch=1,
            grid=(LAYERS,),
            in_specs=[one(64, T), one(T, DW), one(DW, FW), one(1, FW)],
            out_specs=[one(HALF, 128), one(HALF, 128), one(HALF, 128)],
            scratch_shapes=[pltpu.VMEM((128, HALF), I32), pltpu.VMEM((T, FW), F32)],
        ),
        out_shape=[
            jax.ShapeDtypeStruct((LAYERS, HALF, 128), I32),
            jax.ShapeDtypeStruct((LAYERS, HALF, 128), I32),
            jax.ShapeDtypeStruct((LAYERS, HALF, 128), BF),
        ],
        compiler_params=BIG,
        name="encode",
    )(info, active_t, activations, encoder, bias[:, None, :])


def load_decoder(decoder, held, arrived):
    @pl.when(pl.program_id(0) == 0)
    def _():
        @pl.loop(0, PAIRS)
        def _(p):
            pltpu.make_async_copy(decoder.at[p], held.at[p], arrived.at[p]).start()


def rebuild_kernel(info, table, slots, decoder, latent_out, own_out, send_out, total, held, arrived):
    source = pl.program_id(0)
    load_decoder(decoder, held, arrived)

    @pl.when(source == 0)
    def _():
        total[...] = jnp.zeros_like(total)

    def write(half, chunk, part):
        latent_out[0, pl.ds(half * HALF, HALF), pl.ds(chunk * 128, 128)] = part.astype(BF)

    unpack(table[0], slots[0].astype(F32), write)

    @pl.loop(source, LAYERS)
    def _(target):
        p = first_pair(source) + target - source
        pltpu.make_async_copy(decoder.at[p], held.at[p], arrived.at[p]).wait()
        total[target] += jnp.dot(latent_out[0], held[p], preferred_element_type=F32)

    @pl.when(source == LAYERS - 1)
    def _():
        core = info[2]
        for i in range(LAYERS // 2):
            own_out[i] = total[core * 4 + i]
            send_out[i] = total[(1 - core) * 4 + i].astype(BF)


def rebuild(info, table, slots, decoder):
    return pl.pallas_call(
        rebuild_kernel,
        grid_spec=pltpu.PrefetchScalarGridSpec(
            num_scalar_prefetch=1,
            grid=(LAYERS,),
            in_specs=[one(HALF, 128), one(HALF, 128), ANY],
            out_specs=[one(T, FW), whole(4, T, DW), whole(4, T, DW)],
            scratch_shapes=[
                pltpu.VMEM((LAYERS, T, DW), F32),
                pltpu.VMEM((PAIRS, FW, DW), BF),
                pltpu.SemaphoreType.DMA((PAIRS,)),
            ],
        ),
        out_shape=[
            jax.ShapeDtypeStruct((LAYERS, T, FW), BF),
            jax.ShapeDtypeStruct((4, T, DW), F32),
            jax.ShapeDtypeStruct((4, T, DW), BF),
        ],
        compiler_params=BIG,
        name="rebuild",
    )(info, table, slots, decoder)


def grad_act_kernel(columns, errors, decoder, slots_out, total, held, arrived):
    source = pl.program_id(0)
    load_decoder(decoder, held, arrived)
    total[...] = jnp.zeros_like(total)

    @pl.loop(source, LAYERS)
    def _(target):
        p = first_pair(source) + target - source
        pltpu.make_async_copy(decoder.at[p], held.at[p], arrived.at[p]).wait()
        total[...] += lax.dot_general(
            errors[target], held[p], (((1,), (1,)), ((), ())), preferred_element_type=F32
        )

    slots_out[0] = pack(
        lambda half, chunk: total[pl.ds(half * HALF, HALF), pl.ds(chunk * 128, 128)], columns[0]
    ).astype(BF)


def grad_act(columns, errors, decoder):
    return pl.pallas_call(
        grad_act_kernel,
        grid=(LAYERS,),
        in_specs=[one(HALF, 128), whole(LAYERS, T, DW), ANY],
        out_specs=one(HALF, 128),
        out_shape=jax.ShapeDtypeStruct((LAYERS, HALF, 128), BF),
        scratch_shapes=[
            pltpu.VMEM((T, FW), F32),
            pltpu.VMEM((PAIRS, FW, DW), BF),
            pltpu.SemaphoreType.DMA((PAIRS,)),
        ],
        compiler_params=BIG,
        name="grad_act",
    )(columns, errors, decoder)


def grad_decoder_kernel(latent, errors, grad_out, turned, held, sent):
    source = pl.program_id(0)
    turned[...] = latent[0].T

    @pl.loop(source, LAYERS)
    def _(target):
        p = first_pair(source) + target - source
        held[p] = jnp.dot(turned[...], errors[target], preferred_element_type=F32).astype(BF)
        pltpu.make_async_copy(held.at[p], grad_out.at[p], sent.at[p]).start()

    @pl.when(source == LAYERS - 1)
    def _():
        @pl.loop(0, PAIRS)
        def _(p):
            pltpu.make_async_copy(held.at[p], grad_out.at[p], sent.at[p]).wait()


def grad_decoder_of(latent, errors):
    return pl.pallas_call(
        grad_decoder_kernel,
        grid=(LAYERS,),
        in_specs=[one(T, FW), whole(LAYERS, T, DW)],
        out_specs=ANY,
        out_shape=jax.ShapeDtypeStruct((PAIRS, FW, DW), BF),
        scratch_shapes=[
            pltpu.VMEM((FW, T), BF),
            pltpu.VMEM((PAIRS, FW, DW), BF),
            pltpu.SemaphoreType.DMA((PAIRS,)),
        ],
        compiler_params=BIG,
        name="grad_decoder",
    )(latent, errors)


def grad_encoder_kernel(table, slots, acts, grad_out, bias_out, dense):
    def write(half, chunk, part):
        dense[pl.ds(half * HALF, HALF), pl.ds(chunk * 128, 128)] = part.astype(BF)

    unpack(table[0], slots[0].astype(F32), write)
    grad = dense[...]
    grad_out[0] = lax.dot_general(
        acts[0], grad, (((0,), (0,)), ((), ())), preferred_element_type=F32
    ).astype(BF)
    bias_out[0] = jnp.sum(grad.astype(F32), axis=0, keepdims=True)


def grad_encoder_of(table, slots, activations):
    grad, bias = pl.pallas_call(
        grad_encoder_kernel,
        grid=(LAYERS,),
        in_specs=[one(HALF, 128), one(HALF, 128), one(T, DW)],
        out_specs=[one(DW, FW), one(1, FW)],
        out_shape=[
            jax.ShapeDtypeStruct((LAYERS, DW, FW), BF),
            jax.ShapeDtypeStruct((LAYERS, 1, FW), F32),
        ],
        scratch_shapes=[pltpu.VMEM((T, FW), BF)],
        compiler_params=BIG,
        name="grad_encoder",
    )(table, slots, activations)
    return grad, bias[:, 0, :]


CHIPS = [[2 * chip + core for chip in range(8)] for core in range(2)]


def swap_cores(x):
    return lax.ppermute(x, "lat", [(i, i ^ 1) for i in range(16)])


def over_layer(x):
    return lax.all_to_all(x, "layer", 0, 0, tiled=True)


def over_chips(x):
    return lax.all_to_all(x, "lat", 0, 0, axis_index_groups=CHIPS, tiled=True)


def sum_slots(slots):
    own = jnp.sum(over_layer(slots).astype(F32), axis=0).astype(BF)
    return over_layer(jnp.broadcast_to(own[None], slots.shape))


def on_device(activations, targets, encoder, bias, decoder, active):
    lat = lax.axis_index("lat")
    core = lat % 2
    info = jnp.stack(
        [lat * FW, (lax.axis_index("layer") == 0).astype(I32), core]
    ).astype(I32)
    table, columns, partial = encode(info, jnp.swapaxes(active, 1, 2), activations, encoder, bias)
    latent_slots = sum_slots(partial)
    latent, own, send = rebuild(info, table, latent_slots, decoder)
    half = (own + swap_cores(send).astype(F32)).astype(BF).reshape(8, 256, DW)
    mine = jnp.sum(over_chips(half).astype(F32), axis=0)
    first_row = (core * 8 + lat // 2) * 256
    wanted = lax.dynamic_slice_in_dim(targets.reshape(LAYERS * T, DW), first_row, 256)
    error = (mine - wanted.astype(F32)).astype(BF)
    error_half = over_chips(jnp.broadcast_to(error[None], (8, 256, DW)))
    other_half = swap_cores(error_half)
    low = jnp.where(core == 0, error_half, other_half)
    high = jnp.where(core == 0, other_half, error_half)
    errors = jnp.concatenate([low, high]).reshape(LAYERS, T, DW)
    grad_slots = sum_slots(grad_act(columns, errors, decoder))
    grad_decoder = grad_decoder_of(latent, errors)
    grad_encoder, grad_bias = grad_encoder_of(table, grad_slots, activations)
    return (grad_encoder, grad_bias, grad_decoder)


def solution(mesh):
    placed = (
        P(None, None, "layer"),
        P(None, None, "layer"),
        P(None, "layer", "lat"),
        P(None, "lat"),
        P(None, "lat", "layer"),
        P(),
    )
    return jax.shard_map(
        on_device,
        mesh=mesh,
        in_specs=placed,
        out_specs=(P(None, "layer", "lat"), P(None, "lat"), P(None, "lat", "layer")),
        check_vma=False,
    )
```

time: 627 us -> 204 us (0.33)
  waiting for transfers between devices: 317 us -> 20.5 us
  other arithmetic: 157 us -> 6.4 us
  matrix products: 99 us -> 0 us
  Pallas kernels: 0 us -> 95.2 us
  blocking collectives: 0 us -> 60.4 us
  local copies, waits for them, and re-layouts: 32.2 us -> 4.47 us
  starting transfers between devices: 0.63 us -> 15.2 us
  between operations: 15 us -> 0.73 us
    psum x2 -> x0, waiting for transfers between devices: 173 us -> none  [the longest x1 150 us: on_device(): complete = lax.psum(rebuilt, 'lat')]
    reduce_or x1 -> x0, other arithmetic: 142 us -> none  [on_device(): jnp.any(active[source][:, :, None] == columns[None, None, :], axis=1)]
    dot_general x110 -> x0, matrix products: 99 us -> none  [the longest x36 42.3 us: on_device(): lax.dot_general(latent_act[source], errors[target], by_tokens, preferred_...]
    pallas_call x0 -> x5, Pallas kernels: none -> 95.2 us  [the longest x1 28.8 us: rebuild(): pl.pallas_call(rebuild_kernel, grid_spec=pltpu.PrefetchScalarGridSpec(num...]
    reduce_scatter x1 -> x0, waiting for transfers between devices: 94 us -> none  [sum_by_parts(): lax.psum_scatter(padded_to(lines, lax.axis_size(axis)), axis, scatter_dim...]
    all_to_all x0 -> x4, blocking collectives: none -> 60.4 us  [the longest x3 41.3 us: over_layer(): return lax.all_to_all(x, 'layer', 0, 0, tiled=True)]
    all_gather x1 -> x0, waiting for transfers between devices: 49.8 us -> none  [sum_by_parts(): whole = lax.all_gather(own, axis).reshape(-1, *lines.shape[1:])]
    unnamed x36 -> x3, local copies, waits for them, and re-layouts: 19.8 us -> 2.11 us
  transfers between devices with their start and end apart: 4 -> 4, of which waited for: 4 -> 3; matrix products, arithmetic and copies ran while one was open for 33% -> 0% of each run, Pallas kernels for 0% -> 8%
where the time goes in v1:
time: 204 us; the launch traced here: 203 us
  Pallas kernels  95.2 us (47%)
  blocking collectives  60.4 us (30%)
  waiting for transfers between devices  20.5 us (10%)
  starting transfers between devices  15.2 us (7%)
  other arithmetic  6.4 us (3%)
  local copies, waits for them, and re-layouts  4.47 us (2%)
    all_to_all x3, blocking collectives, over_layer(): return lax.all_to_all(x, 'layer', 0, 0, tiled=True)  41.3 us
    pallas_call x1, Pallas kernels, rebuild(): pl.pallas_call(rebuild_kernel, grid_spec=pltpu.PrefetchScalarGridSpec(num...  28.8 us
    pallas_call x1, Pallas kernels, grad_act(): pl.pallas_call(grad_act_kernel, grid=(LAYERS,), in_specs=[one(HALF, 128),...  19.8 us
    all_to_all x1, blocking collectives, over_chips(): return lax.all_to_all(x, 'lat', 0, 0, axis_index_groups=CHIPS, tiled=True)  19.2 us
    pallas_call x1, Pallas kernels, grad_encoder_of(): pl.pallas_call(grad_encoder_kernel, grid=(LAYERS,), in_specs=[one(HALF, 1...  18.4 us
    all_to_all x1, waiting for transfers between devices, over_chips(): return lax.all_to_all(x, 'lat', 0, 0, axis_index_groups=CHIPS, tiled=True)  15.8 us
    pallas_call x1, Pallas kernels, grad_decoder_of(): pl.pallas_call(grad_decoder_kernel, grid=(LAYERS,), in_specs=[one(T, FW),...  15.5 us
    pallas_call x1, Pallas kernels, encode(): pl.pallas_call(encode_kernel, grid_spec=pltpu.PrefetchScalarGridSpec(num_...  12.7 us
  transfers between devices with their start and end apart: 4, of which 3 were waited for; matrix products, arithmetic and copies ran while one was open for 0% of the time, Pallas kernels for 8%

profile of v1, /device:TPU:1, one launch (start us, length us, event | category | flops | bytes accessed | tf_op | source)
XLA Modules:
  0.0 203.0 jit_solution(1830576294612130149)
XLA Ops:
  0.6 1.3 broadcast_in_dim.8.bias
  2.0 0.6 pad_add_fusion.info
  2.6 12.7 %encode.1 = (s32[8,256,128]{2,1,0:T(8,128)}, s32[8,256,128]{2,1,0:T(8,128)}, bf16[8,256,128]{2,1,0:T(8,128)(2,1)}) custom-call(s32[3]{0:T(128)} %pad_add_fusion.info, s32[8,64,512]{2,1,0:T(8,128)} %bitcast.12, bf16[8,512,256]{2,1,0:T(8,128)(2,1)} %acts.3, bf16[8,256,512]{2,1,0:T(8,128)(2,1)} %encoder.1, f32[8,1,512]{2,1,0:T(1,128)} %broadcast_in_dim.8.bias), custom_call_target="tpu_custom_call" | custom-call | tf_op jit(solution)/shard_map/encode/pallas_call | solution.py:127
  15.3 15.6 %all_to_all.30 = bf16[8,256,128]{2,1,0:T(8,128)(2,1)S(1)} all-to-all(bf16[8,256,128]{2,1,0:T(8,128)(2,1)} %get-tuple-element.13), channel_id=1, replica_groups=mesh['layer'=8,'lat'=16] {'layer'}, dimensions={0} | all-to-all | bytes 1048576 | tf_op jit(solution)/shard_map/all_to_all | solution.py:311
  30.8 0.1 reduce_sum.33
  30.9 0.1 broadcast_in_dim.9
  31.0 12.0 %all_to_all.31.slots = bf16[8,256,128]{2,1,0:T(8,128)(2,1)} all-to-all(bf16[8,256,128]{2,1,0:T(8,128)(2,1)S(1)} %broadcast_in_dim.9), channel_id=1, replica_groups=mesh['layer'=8,'lat'=16] {'layer'}, dimensions={0} | all-to-all | bytes 1048576 | tf_op jit(solution)/shard_map/all_to_all | solution.py:311
  43.0 28.8 %rebuild.1 = (bf16[8,512,512]{2,1,0:T(8,128)(2,1)}, f32[4,512,256]{2,1,0:T(8,128)}, bf16[4,512,256]{2,1,0:T(8,128)(2,1)}) custom-call(s32[3]{0:T(128)} %pad_add_fusion.info, s32[8,256,128]{2,1,0:T(8,128)} %get-tuple-element.11.table, bf16[8,256,128]{2,1,0:T(8,128)(2,1)} %all_to_all.31.slots, bf16[36,512,256]{2,1,0:T(8,128)(2,1)} %decoder.3), custom_call_target="tpu_custom_call" | custom-call | tf_op jit(solution)/shard_map/rebuild/pallas_call | solution.py:182
  71.8 2.2 %collective-permute-start = (bf16[4,512,256]{2,1,0:T(8,128)(2,1)}, bf16[4,512,256]{2,1,0:T(8,128)(2,1)S(1)}, u32[]{:S(2)}, u32[]{:S(2)}) collective-permute-start(bf16[4,512,256]{2,1,0:T(8,128)(2,1)} %get-tuple-element.15), channel_id=1, source_target_pairs={{0,1},{1,0},{2,3},{3,2},{4,5},{5,4},{6,7},{7,6},{8,9},{9,8},{10,11... | collective-permute-start | bytes 3145736 | tf_op jit(solution)/shard_map/ppermute | solution.py:307
  74.0 2.5 %collective-permute-done = bf16[4,512,256]{2,1,0:T(8,128)(2,1)S(1)} collective-permute-done((bf16[4,512,256]{2,1,0:T(8,128)(2,1)}, bf16[4,512,256]{2,1,0:T(8,128)(2,1)S(1)}, u32[]{:S(2)}, u32[]{:S(2)}) %collective-permute-start) | collective-permute-done | bytes 1048608 | tf_op jit(solution)/shard_map/ppermute | solution.py:307
  76.5 3.0 %add_convert_fusion = bf16[4,512,256]{2,1,0:T(8,128)(2,1)} fusion(f32[4,512,256]{2,1,0:T(8,128)} %get-tuple-element.14, bf16[4,512,256]{2,1,0:T(8,128)(2,1)S(1)} %collective-permute-done), kind=kLoop, calls=%fused_computation.2 | loop fusion | flops 1572864 | bytes 4194304 | tf_op jit(solution)/shard_map/convert_element_type | solution.py:332
  79.4 7.1 %all-to-all-start.2 = ((bf16[8,256,256]{2,1,0:T(8,128)(2,1)}), bf16[8,256,256]{2,1,0:T(8,128)(2,1)S(1)}, u32[]{:S(2)}, u32[]{:S(2)}) async-start(bf16[8,256,256]{2,1,0:T(8,128)(2,1)} %bitcast.4), calls=%async_computation.2 | async-start | bytes 2097152 | tf_op jit(solution)/shard_map/all_to_all | solution.py:315
  86.5 15.8 %all-to-all-done.2 = bf16[8,256,256]{2,1,0:T(8,128)(2,1)S(1)} async-done(((bf16[8,256,256]{2,1,0:T(8,128)(2,1)}), bf16[8,256,256]{2,1,0:T(8,128)(2,1)S(1)}, u32[]{:S(2)}, u32[]{:S(2)}) %all-to-all-start.2) | async-done | bytes 1048608 | tf_op jit(solution)/shard_map/all_to_all | solution.py:315
  102.3 0.1 convert_reduce_fusion
  102.4 0.9 subtract_convert_fusion
  103.3 0.1 broadcast_in_dim.10
  103.4 19.2 %all_to_all.32 = bf16[8,256,256]{2,1,0:T(8,128)(2,1)S(1)} all-to-all(bf16[8,256,256]{2,1,0:T(8,128)(2,1)S(1)} %broadcast_in_dim.10), channel_id=1, replica_groups={{0,2,4,6,8,10,12,14},{1,3,5,7,9,11,13,15},{16,18,20,22,24,26,28,30},{17..., dimensions={0} | all-to-all | bytes 2097152 | tf_op jit(solution)/shard_map/all_to_all | solution.py:315
  122.6 2.4 %collective-permute-start.1 = (bf16[8,256,256]{2,1,0:T(8,128)(2,1)S(1)}, bf16[8,256,256]{2,1,0:T(8,128)(2,1)S(1)}, u32[]{:S(2)}, u32[]{:S(2)}) collective-permute-start(bf16[8,256,256]{2,1,0:T(8,128)(2,1)S(1)} %all_to_all.32), channel_id=1, source_target_pairs={{0,1},{1,0},{2,3},{3,2},{4,5},{5,4},{6,7},{7,6},{8,9},{9,8},{10,11... | collective-permute-start | bytes 3145736 | tf_op jit(solution)/shard_map/ppermute | solution.py:307
  125.0 2.3 %collective-permute-done.1 = bf16[8,256,256]{2,1,0:T(8,128)(2,1)S(1)} collective-permute-done((bf16[8,256,256]{2,1,0:T(8,128)(2,1)S(1)}, bf16[8,256,256]{2,1,0:T(8,128)(2,1)S(1)}, u32[]{:S(2)}, u32[]{:S(2)}) %collective-permute-start.1) | collective-permute-done | bytes 1048608 | tf_op jit(solution)/shard_map/ppermute | solution.py:307
  127.3 0.1 broadcast_select_fusion.1
  127.5 1.5 pad_maximum_fusion
  129.0 19.8 %grad_act.1 = bf16[8,256,128]{2,1,0:T(8,128)(2,1)} custom-call(s32[8,256,128]{2,1,0:T(8,128)} %get-tuple-element.12.columns, bf16[8,512,256]{2,1,0:T(8,128)(2,1)} %bitcast.10, bf16[36,512,256]{2,1,0:T(8,128)(2,1)} %decoder.3), custom_call_target="tpu_custom_call" | custom-call | tf_op jit(solution)/shard_map/grad_act/pallas_call | solution.py:224
  148.8 13.6 %all_to_all.33 = bf16[8,256,128]{2,1,0:T(8,128)(2,1)S(1)} all-to-all(bf16[8,256,128]{2,1,0:T(8,128)(2,1)} %grad_act.1), channel_id=1, replica_groups=mesh['layer'=8,'lat'=16] {'layer'}, dimensions={0} | all-to-all | bytes 1048576 | tf_op jit(solution)/shard_map/all_to_all | solution.py:311
  162.4 0.1 reduce_sum.35
  162.5 0.9 broadcast_in_dim.11
  163.4 3.5 %all-to-all-start.5 = ((bf16[8,256,128]{2,1,0:T(8,128)(2,1)}), bf16[8,256,128]{2,1,0:T(8,128)(2,1)S(1)}, u32[]{:S(2)}, u32[]{:S(2)}) async-start(bf16[8,256,128]{2,1,0:T(8,128)(2,1)} %broadcast_in_dim.11), calls=%async_computation.5 | async-start | bytes 1048576 | tf_op jit(solution)/shard_map/all_to_all | solution.py:311
  166.9 15.5 %grad_decoder.1 = bf16[36,512,256]{2,1,0:T(8,128)(2,1)} custom-call(bf16[8,512,512]{2,1,0:T(8,128)(2,1)} %get-tuple-element.18.latent, bf16[8,512,256]{2,1,0:T(8,128)(2,1)} %bitcast.11), custom_call_target="tpu_custom_call" | custom-call | tf_op jit(solution)/shard_map/grad_decoder/pallas_call | solution.py:258
  182.4 0.0 all-to-all-done.5.slots
  182.4 0.0 copy-start
  182.4 0.8 copy-done
  183.2 18.4 %grad_encoder.1 = (bf16[8,256,512]{2,1,0:T(8,128)(2,1)}, f32[8,1,512]{2,1,0:T(1,128)}) custom-call(s32[8,256,128]{2,1,0:T(8,128)} %get-tuple-element.11.table, bf16[8,256,128]{2,1,0:T(8,128)(2,1)} %copy-done, bf16[8,512,256]{2,1,0:T(8,128)(2,1)} %acts.3), custom_call_target="tpu_custom_call" | custom-call | tf_op jit(solution)/shard_map/grad_encoder/pallas_call | solution.py:287
  201.6 1.3 copy.11
Async XLA Ops:
  71.8 4.7 %collective-permute-start = (bf16[4,512,256]{2,1,0:T(8,128)(2,1)}, bf16[4,512,256]{2,1,0:T(8,128)(2,1)S(1)}, u32[]{:S(2)}, u32[]{:S(2)}) collective-permute-start(bf16[4,512,256]{2,1,0:T(8,128)(2,1)} %get-tuple-element.15), channel_id=1, source_target_pairs={{0,1},{1,0},{2,3},{3,2},{4,5},{5,4},{6,7},{7,6},{8,9},{9,8},{10,11... | collective-permute-start | bytes 3145736 | tf_op jit(solution)/shard_map/ppermute | solution.py:307
  79.4 22.8 %all-to-all-start.2 = ((bf16[8,256,256]{2,1,0:T(8,128)(2,1)}), bf16[8,256,256]{2,1,0:T(8,128)(2,1)S(1)}, u32[]{:S(2)}, u32[]{:S(2)}) async-start(bf16[8,256,256]{2,1,0:T(8,128)(2,1)} %bitcast.4), calls=%async_computation.2 | async-start | bytes 2097152 | tf_op jit(solution)/shard_map/all_to_all | solution.py:315
  122.6 4.7 %collective-permute-start.1 = (bf16[8,256,256]{2,1,0:T(8,128)(2,1)S(1)}, bf16[8,256,256]{2,1,0:T(8,128)(2,1)S(1)}, u32[]{:S(2)}, u32[]{:S(2)}) collective-permute-start(bf16[8,256,256]{2,1,0:T(8,128)(2,1)S(1)} %all_to_all.32), channel_id=1, source_target_pairs={{0,1},{1,0},{2,3},{3,2},{4,5},{5,4},{6,7},{7,6},{8,9},{9,8},{10,11... | collective-permute-start | bytes 3145736 | tf_op jit(solution)/shard_map/ppermute | solution.py:307
  163.4 19.0 %all-to-all-start.5 = ((bf16[8,256,128]{2,1,0:T(8,128)(2,1)}), bf16[8,256,128]{2,1,0:T(8,128)(2,1)S(1)}, u32[]{:S(2)}, u32[]{:S(2)}) async-start(bf16[8,256,128]{2,1,0:T(8,128)(2,1)} %broadcast_in_dim.11), calls=%async_computation.5 | async-start | bytes 1048576 | tf_op jit(solution)/shard_map/all_to_all | solution.py:311
  182.4 0.8 copy-start

commit v2 on v0

v2 whole, which is shorter than its diff:
```python
import jax
import jax.numpy as jnp
from jax import lax
from jax.experimental import pallas as pl
from jax.experimental.pallas import tpu as pltpu
from jax.sharding import PartitionSpec as P

LAYERS = 8
T = 512
HALF = T // 2
DW = 256
FW = 512
ROWS = 256
PAIRS = LAYERS * (LAYERS + 1) // 2
BF = jnp.bfloat16
F32 = jnp.float32
I32 = jnp.int32
ANY = pl.BlockSpec(memory_space=pl.ANY)
HELD = pl.BlockSpec(memory_space=pltpu.VMEM)


def params(steps=0):
    return pltpu.CompilerParams(
        dimension_semantics=("arbitrary",) * steps, vmem_limit_bytes=60 * 1024 * 1024
    )


def first_pair(source):
    return source * LAYERS - source * (source - 1) // 2


def take(x, index):
    return jnp.take_along_axis(x, index, axis=1)


def lanes(rows):
    return lax.broadcasted_iota(I32, (rows, 128), 1)


def right(x, by):
    return lax.shift_right_logical(x, jnp.full_like(x, by) if isinstance(by, int) else by)


def slot_columns(table):
    lane = lanes(table.shape[0])
    base = lane & 64
    r = lane & 63
    at = jnp.zeros_like(r)
    entry = take(table, base)
    for step in (16, 8, 4, 2, 1):
        found = take(table, base + at + step)
        good = right(found, 16) <= r
        at = jnp.where(good, at + step, at)
        entry = jnp.where(good, found, entry)
    k = r - right(entry, 16)
    left = entry & 0xFFFF
    spot = jnp.zeros_like(r)
    for step in (8, 4, 2, 1):
        low = lax.population_count(left & ((1 << step) - 1))
        good = k >= low
        k = jnp.where(good, k - low, k)
        left = jnp.where(good, right(left, step), left)
        spot = jnp.where(good, spot + step, spot)
    return at * 16 + spot


def pack(dense, columns_at, write):
    lane = lanes(ROWS)

    @pl.loop(0, HALF // ROWS)
    def _(block):
        row = pl.multiple_of(block * ROWS, ROWS)
        columns = columns_at(row)
        within = columns & 127
        chunk_of = right(columns, 7)
        packed = None
        for chunk in range(FW // 128):
            part = pl.ds(chunk * 128, 128)
            low = take(dense[pl.ds(row, ROWS), part], within)
            high = take(dense[pl.ds(row + HALF, ROWS), part], within)
            picked = jnp.where(lane < 64, low, high)
            packed = picked if packed is None else jnp.where(chunk_of == chunk, picked, packed)
        write(row, packed.astype(BF))


def unpack(ranks, slots, dense):
    @pl.loop(0, HALF // ROWS)
    def _(block):
        row = pl.multiple_of(block * ROWS, ROWS)
        values = slots[pl.ds(row, ROWS), :].astype(F32)
        for half in range(2):
            for chunk in range(FW // 128):
                place = (pl.ds(row + half * HALF, ROWS), pl.ds(chunk * 128, 128))
                rank = ranks[place]
                value = jnp.where(rank >= 0, take(values, rank & 127), 0.0)
                dense[place] = value.astype(BF)


def encode_kernel(active, acts, encoder, bias, table_out, columns_out, slots_out, rows, dense):
    layer = pl.program_id(0)
    rel = active[0] - lax.axis_index("lat") * FW
    high = lax.shift_right_arithmetic(rel, jnp.full_like(rel, 5))
    bits = lax.shift_left(jnp.full_like(rel, 1), rel & 31)

    @pl.when(layer == 0)
    def _():
        rows[...] = jnp.zeros_like(rows)

    before = jnp.zeros((1, T), I32)
    for word in range(16):
        marked = jnp.where(high == word, bits, 0)
        folded = marked[0:8]
        for k in range(8, 64, 8):
            folded = folded | marked[k : k + 8]
        both = jnp.sum(folded, axis=0, keepdims=True)
        for part in range(2):
            piece = both & 0xFFFF if part == 0 else right(both, 16)
            entry = piece | lax.shift_left(before, jnp.full_like(before, 16))
            before = before + lax.population_count(piece)
            for half in range(2):
                at = 64 * half + 2 * word + part
                rows[at : at + 1, :] = entry[:, half * HALF : (half + 1) * HALF]
    table_out[0] = rows[...].T

    @pl.loop(0, HALF // ROWS)
    def _(block):
        at = (0, pl.ds(pl.multiple_of(block * ROWS, ROWS), ROWS), slice(None))
        columns_out[at] = slot_columns(table_out[at])

    added = jnp.where(lax.axis_index("layer") == 0, 1.0, 0.0).astype(F32)
    value = jnp.dot(acts[0], encoder[0], preferred_element_type=F32)
    dense[...] = value + bias[pl.ds(layer, 1), :] * added

    def write(row, packed):
        slots_out[0, pl.ds(row, ROWS), :] = packed

    pack(dense, lambda row: columns_out[0, pl.ds(row, ROWS), :], write)


def one(*shape):
    return pl.BlockSpec((1,) + shape, lambda i: (i,) + (0,) * len(shape))


def whole(*shape):
    return pl.BlockSpec(shape, lambda i: (0,) * len(shape))


def encode(active_t, activations, encoder, bias):
    return pl.pallas_call(
        encode_kernel,
        grid=(LAYERS,),
        in_specs=[one(64, T), one(T, DW), one(DW, FW), whole(LAYERS, FW)],
        out_specs=[one(HALF, 128), one(HALF, 128), one(HALF, 128)],
        out_shape=[
            jax.ShapeDtypeStruct((LAYERS, HALF, 128), I32),
            jax.ShapeDtypeStruct((LAYERS, HALF, 128), I32),
            jax.ShapeDtypeStruct((LAYERS, HALF, 128), BF),
        ],
        scratch_shapes=[pltpu.VMEM((128, HALF), I32), pltpu.VMEM((T, FW), F32)],
        compiler_params=params(1),
        name="encode",
    )(active_t, activations, encoder, bias)


def ranks_kernel(table, acts, ranks_out, turned_out, ranks, turned, sent):
    lane = lanes(ROWS)
    bit = lane & 15
    below = lax.shift_left(jnp.full_like(bit, 1), bit) - 1

    @pl.loop(0, LAYERS)
    def _(layer):
        turned[layer] = acts[layer].T

        @pl.loop(0, HALF // ROWS)
        def _(block):
            row = pl.multiple_of(block * ROWS, ROWS)
            entries = table[layer, pl.ds(row, ROWS), :]
            for half in range(2):
                for chunk in range(FW // 128):
                    entry = take(entries, 64 * half + 8 * chunk + right(lane, 4))
                    rank = right(entry, 16) + lax.population_count(entry & below) + 64 * half
                    hit = (right(entry, bit) & 1) == 1
                    place = (layer, pl.ds(row + half * HALF, ROWS), pl.ds(chunk * 128, 128))
                    ranks[place] = jnp.where(hit, rank, -1)

        pltpu.make_async_copy(ranks.at[layer], ranks_out.at[layer], sent.at[layer]).start()
        pltpu.make_async_copy(turned.at[layer], turned_out.at[layer], sent.at[LAYERS + layer]).start()

    @pl.loop(0, LAYERS)
    def _(layer):
        pltpu.make_async_copy(ranks.at[layer], ranks_out.at[layer], sent.at[layer]).wait()
        pltpu.make_async_copy(turned.at[layer], turned_out.at[layer], sent.at[LAYERS + layer]).wait()


def ranks_of(table, activations):
    return pl.pallas_call(
        ranks_kernel,
        in_specs=[HELD, HELD],
        out_specs=[ANY, ANY],
        out_shape=[
            jax.ShapeDtypeStruct((LAYERS, T, FW), I32),
            jax.ShapeDtypeStruct((LAYERS, DW, T), BF),
        ],
        scratch_shapes=[
            pltpu.VMEM((LAYERS, T, FW), I32),
            pltpu.VMEM((LAYERS, DW, T), BF),
            pltpu.SemaphoreType.DMA((2 * LAYERS,)),
        ],
        compiler_params=params(),
        cost_estimate=pl.CostEstimate(flops=4 * 10**9, transcendentals=0, bytes_accessed=12 * 2**20),
        name="ranks",
    )(table, activations)


def each(count, copy, act):
    @pl.loop(0, count)
    def _(i):
        getattr(copy(i), act)()


def rebuild_kernel(ranks_in, slots, decoder, latent_out, own_out, send_out, ranks, latent, total, stage, held, rank_sem, pair_sem, out_sem):
    core = lax.axis_index("lat") % 2

    def load_ranks(layer):
        return pltpu.make_async_copy(ranks_in.at[layer], ranks.at[layer], rank_sem.at[layer])

    def load_pair(p):
        return pltpu.make_async_copy(decoder.at[p], held.at[p], pair_sem.at[p])

    def send_latent(layer):
        return pltpu.make_async_copy(latent.at[layer], latent_out.at[layer], out_sem.at[layer])

    def send_own(i):
        return pltpu.make_async_copy(total.at[core * 4 + i], own_out.at[i], out_sem.at[LAYERS + i])

    def send_other(i):
        return pltpu.make_async_copy(stage.at[i], send_out.at[i], out_sem.at[LAYERS + 4 + i])

    load_ranks(0).start()

    @pl.loop(0, LAYERS)
    def _(source):
        @pl.when(source + 1 < LAYERS)
        def _():
            load_ranks(source + 1).start()

        @pl.loop(source, LAYERS)
        def _(target):
            load_pair(first_pair(source) + target - source).start()

    total[...] = jnp.zeros_like(total)

    @pl.loop(0, LAYERS)
    def _(source):
        load_ranks(source).wait()
        unpack(ranks.at[source], slots.at[source], latent.at[source])
        send_latent(source).start()

        @pl.loop(source, LAYERS)
        def _(target):
            p = first_pair(source) + target - source
            load_pair(p).wait()
            total[target] += jnp.dot(latent[source], held[p], preferred_element_type=F32)

        spot = source % 4

        @pl.when(source // 4 == core)
        def _():
            send_own(spot).start()

        @pl.when(source // 4 != core)
        def _():
            stage[spot] = total[source].astype(BF)
            send_other(spot).start()

    each(LAYERS, send_latent, "wait")
    each(4, send_own, "wait")
    each(4, send_other, "wait")


def rebuild(ranks, slots, decoder):
    return pl.pallas_call(
        rebuild_kernel,
        in_specs=[ANY, HELD, ANY],
        out_specs=[ANY, ANY, ANY],
        out_shape=[
            jax.ShapeDtypeStruct((LAYERS, T, FW), BF),
            jax.ShapeDtypeStruct((4, T, DW), F32),
            jax.ShapeDtypeStruct((4, T, DW), BF),
        ],
        scratch_shapes=[
            pltpu.VMEM((LAYERS, T, FW), I32),
            pltpu.VMEM((LAYERS, T, FW), BF),
            pltpu.VMEM((LAYERS, T, DW), F32),
            pltpu.VMEM((4, T, DW), BF),
            pltpu.VMEM((PAIRS, FW, DW), BF),
            pltpu.SemaphoreType.DMA((LAYERS,)),
            pltpu.SemaphoreType.DMA((PAIRS,)),
            pltpu.SemaphoreType.DMA((2 * LAYERS,)),
        ],
        compiler_params=params(),
        name="rebuild",
    )(ranks, slots, decoder)


def error_loads(mine, other, errors, sems):
    core = lax.axis_index("lat") % 2

    def load(which):
        def at(i):
            spot = (core if which == 0 else 1 - core) * 4 + i
            source = mine if which == 0 else other
            return pltpu.make_async_copy(source.at[i], errors.at[spot], sems.at[which * 4 + i])

        return at

    return load(0), load(1)


def grad_act_kernel(columns, mine, other, decoder, slots_out, errors, total, held, error_sem, pair_sem):
    loads = error_loads(mine, other, errors, error_sem)

    def load_pair(p):
        return pltpu.make_async_copy(decoder.at[p], held.at[p], pair_sem.at[p])

    for load in loads:
        each(4, load, "start")
    each(PAIRS, load_pair, "start")
    for load in loads:
        each(4, load, "wait")

    for source in range(LAYERS):
        for target in range(source, LAYERS):
            p = first_pair(source) + target - source
            load_pair(p).wait()
            part = lax.dot_general(
                errors[target], held[p], (((1,), (1,)), ((), ())), preferred_element_type=F32
            )
            summed = part if target == source else summed + part
        total[...] = summed

        def write(row, packed):
            slots_out[source, pl.ds(row, ROWS), :] = packed

        pack(total, lambda row: columns[source, pl.ds(row, ROWS), :], write)


def grad_act(columns, mine, other, decoder):
    return pl.pallas_call(
        grad_act_kernel,
        in_specs=[HELD, ANY, ANY, ANY],
        out_specs=HELD,
        out_shape=jax.ShapeDtypeStruct((LAYERS, HALF, 128), BF),
        scratch_shapes=[
            pltpu.VMEM((LAYERS, T, DW), BF),
            pltpu.VMEM((T, FW), F32),
            pltpu.VMEM((PAIRS, FW, DW), BF),
            pltpu.SemaphoreType.DMA((LAYERS,)),
            pltpu.SemaphoreType.DMA((PAIRS,)),
        ],
        compiler_params=params(),
        name="grad_act",
    )(columns, mine, other, decoder)


def grad_decoder_part(latent, mine, other, begin, end, earlier=None):
    first, last = first_pair(begin), first_pair(end)
    layers = end - begin

    def kernel(*refs):
        latent_in, mine_in, other_in = refs[:3]
        grad_out, latents, errors, turned, held, latent_sem, error_sem, sent = refs[-8:]
        loads = error_loads(mine_in, other_in, errors, error_sem)

        def load_latent(i):
            return pltpu.make_async_copy(latent_in.at[begin + i], latents.at[i], latent_sem.at[i])

        def send(i):
            return pltpu.make_async_copy(held.at[i], grad_out.at[first + i], sent.at[i])

        load_latent(0).start()
        for load in loads:
            each(4, load, "start")

        @pl.loop(1, layers)
        def _(i):
            load_latent(i).start()

        for load in loads:
            each(4, load, "wait")

        for i in range(layers):
            source = begin + i
            load_latent(i).wait()
            turned[...] = latents[i].T
            for target in range(source, LAYERS):
                at = first_pair(source) + target - source - first
                held[at] = jnp.dot(turned[...], errors[target], preferred_element_type=F32).astype(BF)
                send(at).start()

        each(last - first, send, "wait")

    operands = (latent, mine, other) + (() if earlier is None else (earlier,))
    return pl.pallas_call(
        kernel,
        in_specs=[ANY] * len(operands),
        out_specs=ANY,
        out_shape=jax.ShapeDtypeStruct((PAIRS, FW, DW), BF),
        scratch_shapes=[
            pltpu.VMEM((layers, T, FW), BF),
            pltpu.VMEM((LAYERS, T, DW), BF),
            pltpu.VMEM((FW, T), BF),
            pltpu.VMEM((last - first, FW, DW), BF),
            pltpu.SemaphoreType.DMA((layers,)),
            pltpu.SemaphoreType.DMA((LAYERS,)),
            pltpu.SemaphoreType.DMA((last - first,)),
        ],
        input_output_aliases={} if earlier is None else {3: 0},
        compiler_params=params(),
        cost_estimate=pl.CostEstimate(
            flops=2 * (last - first) * T * FW * DW,
            transcendentals=0,
            bytes_accessed=2 * (last - first) * FW * DW,
        ),
        name=f"grad_decoder_{begin}",
    )(*operands)


def grad_encoder_kernel(ranks_in, slots, turned_in, grad_out, bias_out, ranks, turned, dense, grad, rank_sem, turned_sem, sent):
    def load_ranks(layer):
        return pltpu.make_async_copy(ranks_in.at[layer], ranks.at[layer], rank_sem.at[layer])

    def load_turned(layer):
        return pltpu.make_async_copy(turned_in.at[layer], turned.at[layer], turned_sem.at[layer])

    def send(layer):
        return pltpu.make_async_copy(grad.at[layer], grad_out.at[layer], sent.at[layer])

    @pl.loop(0, LAYERS)
    def _(layer):
        load_ranks(layer).start()
        load_turned(layer).start()

    @pl.loop(0, LAYERS)
    def _(layer):
        load_ranks(layer).wait()
        unpack(ranks.at[layer], slots.at[layer], dense.at[layer])

    for layer in range(LAYERS):
        load_turned(layer).wait()
        grad[layer] = jnp.dot(turned[layer], dense[layer], preferred_element_type=F32).astype(BF)
        send(layer).start()
        bias_out[pl.ds(layer, 1), :] = jnp.sum(dense[layer].astype(F32), axis=0, keepdims=True)

    each(LAYERS, send, "wait")


def grad_encoder_of(ranks, slots, turned):
    return pl.pallas_call(
        grad_encoder_kernel,
        in_specs=[ANY, HELD, ANY],
        out_specs=[ANY, HELD],
        out_shape=[
            jax.ShapeDtypeStruct((LAYERS, DW, FW), BF),
            jax.ShapeDtypeStruct((LAYERS, FW), F32),
        ],
        scratch_shapes=[
            pltpu.VMEM((LAYERS, T, FW), I32),
            pltpu.VMEM((LAYERS, DW, T), BF),
            pltpu.VMEM((LAYERS, T, FW), BF),
            pltpu.VMEM((LAYERS, DW, FW), BF),
            pltpu.SemaphoreType.DMA((LAYERS,)),
            pltpu.SemaphoreType.DMA((LAYERS,)),
            pltpu.SemaphoreType.DMA((LAYERS,)),
        ],
        compiler_params=params(),
        name="grad_encoder",
    )(ranks, slots, turned)


CHIPS = [[2 * chip + core for chip in range(8)] for core in range(2)]


def swap_cores(x):
    return lax.ppermute(x, "lat", [(i, i ^ 1) for i in range(16)])


def over_layer(x):
    return lax.all_to_all(x, "layer", 0, 0, tiled=True)


def over_chips(x):
    return lax.all_to_all(x, "lat", 0, 0, axis_index_groups=CHIPS, tiled=True)


def sum_slots(slots, beside):
    own = jnp.sum(over_layer(slots).astype(F32), axis=0).astype(BF)
    own, beside = lax.optimization_barrier((own, beside))
    return over_layer(jnp.broadcast_to(own[None], slots.shape)), beside


def on_device(activations, targets, encoder, bias, decoder, active):
    lat = lax.axis_index("lat")
    first_row = ((lat % 2) * 8 + lat // 2) * 256
    table, columns, partial = encode(jnp.swapaxes(active, 1, 2), activations, encoder, bias)
    ranks, turned = ranks_of(table, activations)
    latent_slots, ranks = sum_slots(partial, ranks)
    latent, own, send = rebuild(ranks, latent_slots, decoder)
    half = (own + swap_cores(send).astype(F32)).astype(BF).reshape(8, 256, DW)
    total = jnp.sum(over_chips(half).astype(F32), axis=0)
    wanted = lax.dynamic_slice_in_dim(targets.reshape(LAYERS * T, DW), first_row, 256)
    error = (total - wanted.astype(F32)).astype(BF)
    mine = over_chips(jnp.broadcast_to(error[None], (8, 256, DW))).reshape(4, T, DW)
    other = swap_cores(mine)
    grad_slots = grad_act(columns, mine, other, decoder)
    grad_decoder = grad_decoder_part(latent, mine, other, 0, 2)
    grad_slots, grad_decoder = sum_slots(grad_slots, grad_decoder)
    grad_decoder = grad_decoder_part(latent, mine, other, 2, LAYERS, grad_decoder)
    grad_encoder, grad_bias = grad_encoder_of(ranks, grad_slots, turned)
    return (grad_encoder, grad_bias, grad_decoder)


def solution(mesh):
    placed = (
        P(None, None, "layer"),
        P(None, None, "layer"),
        P(None, "layer", "lat"),
        P(None, "lat"),
        P(None, "lat", "layer"),
        P(),
    )
    return jax.shard_map(
        on_device,
        mesh=mesh,
        in_specs=placed,
        out_specs=(P(None, "layer", "lat"), P(None, "lat"), P(None, "lat", "layer")),
        check_vma=False,
    )
```

time: 627 us -> 177 us (0.28)
  waiting for transfers between devices: 317 us -> 31.6 us
  other arithmetic: 157 us -> 4.17 us
  matrix products: 99 us -> 0 us
  Pallas kernels: 0 us -> 80.4 us
  blocking collectives: 0 us -> 31.4 us
  local copies, waits for them, and re-layouts: 32.2 us -> 2.82 us
  starting transfers between devices: 0.63 us -> 24.9 us
  between operations: 15 us -> 0.89 us
    psum x2 -> x0, waiting for transfers between devices: 173 us -> none  [the longest x1 150 us: on_device(): complete = lax.psum(rebuilt, 'lat')]
    reduce_or x1 -> x0, other arithmetic: 142 us -> none  [on_device(): jnp.any(active[source][:, :, None] == columns[None, None, :], axis=1)]
    dot_general x110 -> x0, matrix products: 99 us -> none  [the longest x36 42.3 us: on_device(): lax.dot_general(latent_act[source], errors[target], by_tokens, preferred_...]
    reduce_scatter x1 -> x0, waiting for transfers between devices: 94 us -> none  [sum_by_parts(): lax.psum_scatter(padded_to(lines, lax.axis_size(axis)), axis, scatter_dim...]
    pallas_call x0 -> x7, Pallas kernels: none -> 80.4 us  [the longest x1 21 us: rebuild(): pl.pallas_call(rebuild_kernel, in_specs=[ANY, HELD, ANY], out_specs=[ANY,...]
    all_gather x1 -> x0, waiting for transfers between devices: 49.8 us -> none  [sum_by_parts(): whole = lax.all_gather(own, axis).reshape(-1, *lines.shape[1:])]
    all_to_all x0 -> x2, blocking collectives: none -> 31.4 us  [the longest x1 19.2 us: over_chips(): return lax.all_to_all(x, 'lat', 0, 0, axis_index_groups=CHIPS, tiled=True)]
    all_to_all x0 -> x4, waiting for transfers between devices: none -> 26.8 us  [the longest x1 15.8 us: over_chips(): return lax.all_to_all(x, 'lat', 0, 0, axis_index_groups=CHIPS, tiled=True)]
  transfers between devices with their start and end apart: 4 -> 6, of which waited for: 4 -> 6; matrix products, arithmetic and copies ran while one was open for 33% -> 0% of each run, Pallas kernels for 0% -> 11%
where the time goes in v2:
time: 177 us; the launch traced here: 176 us
  Pallas kernels  80.4 us (45%)
  waiting for transfers between devices  31.6 us (18%)
  blocking collectives  31.4 us (18%)
  starting transfers between devices  24.9 us (14%)
  other arithmetic  4.17 us (2%)
  local copies, waits for them, and re-layouts  2.82 us (2%)
    pallas_call x1, Pallas kernels, rebuild(): pl.pallas_call(rebuild_kernel, in_specs=[ANY, HELD, ANY], out_specs=[ANY,...  21 us
    all_to_all x1, blocking collectives, over_chips(): return lax.all_to_all(x, 'lat', 0, 0, axis_index_groups=CHIPS, tiled=True)  19.2 us
    all_to_all x1, waiting for transfers between devices, over_chips(): return lax.all_to_all(x, 'lat', 0, 0, axis_index_groups=CHIPS, tiled=True)  15.8 us
    pallas_call x1, Pallas kernels, grad_act(): pl.pallas_call(grad_act_kernel, in_specs=[HELD, ANY, ANY, ANY], out_specs...  14.4 us
    all_to_all x3, starting transfers between devices, over_layer(): return lax.all_to_all(x, 'layer', 0, 0, tiled=True)  13.5 us
    pallas_call x1, Pallas kernels, encode(): pl.pallas_call(encode_kernel, grid=(LAYERS,), in_specs=[one(64, T), one(T...  13.1 us
    pallas_call x2, Pallas kernels, grad_decoder_part(): pl.pallas_call(kernel, in_specs=[ANY] * len(operands), out_specs=ANY, out...  12.7 us
    pallas_call x1, Pallas kernels, grad_encoder_of(): pl.pallas_call(grad_encoder_kernel, in_specs=[ANY, HELD, ANY], out_specs=...  12.6 us
  transfers between devices with their start and end apart: 6, of which 6 were waited for; matrix products, arithmetic and copies ran while one was open for 0% of the time, Pallas kernels for 11%

profile of v2, /device:TPU:1, one launch (start us, length us, event | category | flops | bytes accessed | tf_op | source)
XLA Modules:
  0.0 176.2 jit_solution(17164575222773706717)
XLA Ops:
  0.6 13.1 %encode.1 = (s32[8,256,128]{2,1,0:T(8,128)}, s32[8,256,128]{2,1,0:T(8,128)}, bf16[8,256,128]{2,1,0:T(8,128)(2,1)}) custom-call(s32[8,64,512]{2,1,0:T(8,128)} %bitcast.8, bf16[8,512,256]{2,1,0:T(8,128)(2,1)} %acts.3, bf16[8,256,512]{2,1,0:T(8,128)(2,1)} %encoder.1, f32[8,512]{1,0:T(8,128)} %bias.1), custom_call_target="tpu_custom_call" | custom-call | tf_op jit(solution)/shard_map/encode/pallas_call | solution.py:149
  13.7 6.4 %all-to-all-start = ((bf16[8,256,128]{2,1,0:T(8,128)(2,1)}), bf16[8,256,128]{2,1,0:T(8,128)(2,1)S(1)}, u32[]{:S(2)}, u32[]{:S(2)}) async-start(bf16[8,256,128]{2,1,0:T(8,128)(2,1)} %get-tuple-element.17), calls=%async_computation | async-start | bytes 1048576 | tf_op jit(solution)/shard_map/all_to_all | solution.py:489
  20.1 6.7 %ranks.1 = (s32[8,512,512]{2,1,0:T(8,128)}, bf16[8,256,512]{2,1,0:T(8,128)(2,1)}) custom-call(s32[8,256,128]{2,1,0:T(8,128)} %get-tuple-element.18.table, bf16[8,512,256]{2,1,0:T(8,128)(2,1)} %acts.3), custom_call_target="tpu_custom_call" | custom-call | flops 4000000000 | bytes 12582912 | tf_op jit(solution)/shard_map/ranks/pallas_call | solution.py:196
  26.8 3.6 %all-to-all-done = bf16[8,256,128]{2,1,0:T(8,128)(2,1)S(1)} async-done(((bf16[8,256,128]{2,1,0:T(8,128)(2,1)}), bf16[8,256,128]{2,1,0:T(8,128)(2,1)S(1)}, u32[]{:S(2)}, u32[]{:S(2)}) %all-to-all-start) | async-done | bytes 524320 | tf_op jit(solution)/shard_map/all_to_all | solution.py:489
  30.4 0.1 reduce_sum.33
  30.4 0.1 broadcast_in_dim.6
  30.5 12.2 %all_to_all.30.slots = bf16[8,256,128]{2,1,0:T(8,128)(2,1)} all-to-all(bf16[8,256,128]{2,1,0:T(8,128)(2,1)S(1)} %broadcast_in_dim.6), channel_id=1, replica_groups=mesh['layer'=8,'lat'=16] {'layer'}, dimensions={0} | all-to-all | bytes 1048576 | tf_op jit(solution)/shard_map/all_to_all | solution.py:489
  42.7 21.0 %rebuild.1 = (bf16[8,512,512]{2,1,0:T(8,128)(2,1)}, f32[4,512,256]{2,1,0:T(8,128)}, bf16[4,512,256]{2,1,0:T(8,128)(2,1)}) custom-call(s32[8,512,512]{2,1,0:T(8,128)} %get-tuple-element.20.ranks_in, bf16[8,256,128]{2,1,0:T(8,128)(2,1)} %all_to_all.30.slots, bf16[36,512,256]{2,1,0:T(8,128)(2,1)} %decoder.3), custom_call_target="tpu_custom_call" | custom-call | tf_op jit(solution)/shard_map/rebuild/pallas_call | solution.py:282
  63.7 1.9 %collective-permute-start = (bf16[4,512,256]{2,1,0:T(8,128)(2,1)}, bf16[4,512,256]{2,1,0:T(8,128)(2,1)S(1)}, u32[]{:S(2)}, u32[]{:S(2)}) collective-permute-start(bf16[4,512,256]{2,1,0:T(8,128)(2,1)} %get-tuple-element.24), channel_id=1, source_target_pairs={{0,1},{1,0},{2,3},{3,2},{4,5},{5,4},{6,7},{7,6},{8,9},{9,8},{10,11... | collective-permute-start | bytes 3145736 | tf_op jit(solution)/shard_map/ppermute | solution.py:485
  65.6 2.5 %collective-permute-done = bf16[4,512,256]{2,1,0:T(8,128)(2,1)S(1)} collective-permute-done((bf16[4,512,256]{2,1,0:T(8,128)(2,1)}, bf16[4,512,256]{2,1,0:T(8,128)(2,1)S(1)}, u32[]{:S(2)}, u32[]{:S(2)}) %collective-permute-start) | collective-permute-done | bytes 1048608 | tf_op jit(solution)/shard_map/ppermute | solution.py:485
  68.1 2.9 %add_convert_fusion = bf16[4,512,256]{2,1,0:T(8,128)(2,1)} fusion(f32[4,512,256]{2,1,0:T(8,128)} %get-tuple-element.23, bf16[4,512,256]{2,1,0:T(8,128)(2,1)S(1)} %collective-permute-done), kind=kLoop, calls=%fused_computation.1 | loop fusion | flops 1572864 | bytes 4194304 | tf_op jit(solution)/shard_map/convert_element_type | solution.py:509
  71.1 7.0 %all-to-all-start.2 = ((bf16[8,256,256]{2,1,0:T(8,128)(2,1)}), bf16[8,256,256]{2,1,0:T(8,128)(2,1)S(1)}, u32[]{:S(2)}, u32[]{:S(2)}) async-start(bf16[8,256,256]{2,1,0:T(8,128)(2,1)} %bitcast.1), calls=%async_computation.2 | async-start | bytes 2097152 | tf_op jit(solution)/shard_map/all_to_all | solution.py:493
  78.1 15.8 %all-to-all-done.2 = bf16[8,256,256]{2,1,0:T(8,128)(2,1)S(1)} async-done(((bf16[8,256,256]{2,1,0:T(8,128)(2,1)}), bf16[8,256,256]{2,1,0:T(8,128)(2,1)S(1)}, u32[]{:S(2)}, u32[]{:S(2)}) %all-to-all-start.2) | async-done | bytes 1048608 | tf_op jit(solution)/shard_map/all_to_all | solution.py:493
  93.9 0.1 convert_reduce_fusion
  94.0 0.9 subtract_convert_fusion
  94.9 0.1 broadcast_in_dim.7
  95.0 19.2 %all_to_all.31 = bf16[8,256,256]{2,1,0:T(8,128)(2,1)S(1)} all-to-all(bf16[8,256,256]{2,1,0:T(8,128)(2,1)S(1)} %broadcast_in_dim.7), channel_id=1, replica_groups={{0,2,4,6,8,10,12,14},{1,3,5,7,9,11,13,15},{16,18,20,22,24,26,28,30},{17..., dimensions={0} | all-to-all | bytes 2097152 | tf_op jit(solution)/shard_map/all_to_all | solution.py:493
  114.2 0.0 copy-start
  114.2 2.4 %collective-permute-start.1 = (bf16[4,512,256]{2,1,0:T(8,128)(2,1)S(1)}, bf16[4,512,256]{2,1,0:T(8,128)(2,1)S(1)}, u32[]{:S(2)}, u32[]{:S(2)}) collective-permute-start(bf16[4,512,256]{2,1,0:T(8,128)(2,1)S(1)} %bitcast.4), channel_id=1, source_target_pairs={{0,1},{1,0},{2,3},{3,2},{4,5},{5,4},{6,7},{7,6},{8,9},{9,8},{10,11... | collective-permute-start | bytes 3145736 | tf_op jit(solution)/shard_map/ppermute | solution.py:485
  116.6 2.3 %collective-permute-done.1.other.refs_2_ = bf16[4,512,256]{2,1,0:T(8,128)(2,1)S(1)} collective-permute-done((bf16[4,512,256]{2,1,0:T(8,128)(2,1)S(1)}, bf16[4,512,256]{2,1,0:T(8,128)(2,1)S(1)}, u32[]{:S(2)}, u32[]{:S(2)}) %collective-permute-start.1) | collective-permute-done | bytes 1048608 | tf_op jit(solution)/shard_map/ppermute | solution.py:485
  118.9 0.0 copy-start.1
  118.9 0.0 copy-done
  118.9 1.0 copy-done.1
  119.9 14.4 %grad_act.1 = bf16[8,256,128]{2,1,0:T(8,128)(2,1)} custom-call(s32[8,256,128]{2,1,0:T(8,128)} %get-tuple-element.21.columns, bf16[4,512,256]{2,1,0:T(8,128)(2,1)} %bitcast.5, bf16[4,512,256]{2,1,0:T(8,128)(2,1)} %copy-done.1, bf16[36,512,256]{2,1,0:T(8,128)(2,1)} %decoder.3), custom_call_target="tpu_custom_call" | custom-call | tf_op jit(solution)/shard_map/grad_act/pallas_call | solution.py:349
  134.3 3.7 %all-to-all-start.4 = ((bf16[8,256,128]{2,1,0:T(8,128)(2,1)}), bf16[8,256,128]{2,1,0:T(8,128)(2,1)S(1)}, u32[]{:S(2)}, u32[]{:S(2)}) async-start(bf16[8,256,128]{2,1,0:T(8,128)(2,1)} %grad_act.1), calls=%async_computation.4 | async-start | bytes 1048576 | tf_op jit(solution)/shard_map/all_to_all | solution.py:489
  138.0 5.4 %grad_decoder_0.1.refs_3_ = bf16[36,512,256]{2,1,0:T(8,128)(2,1)} custom-call(bf16[8,512,512]{2,1,0:T(8,128)(2,1)} %get-tuple-element.25.refs_0_, bf16[4,512,256]{2,1,0:T(8,128)(2,1)} %bitcast.6, bf16[4,512,256]{2,1,0:T(8,128)(2,1)} %copy-done.1), custom_call_target="tpu_custom_call" | custom-call | flops 2013265920 | bytes 3932160 | tf_op jit(solution)/shard_map/grad_decoder_0/pallas_call | solution.py:404
  143.4 4.6 %all-to-all-done.4 = bf16[8,256,128]{2,1,0:T(8,128)(2,1)S(1)} async-done(((bf16[8,256,128]{2,1,0:T(8,128)(2,1)}), bf16[8,256,128]{2,1,0:T(8,128)(2,1)S(1)}, u32[]{:S(2)}, u32[]{:S(2)}) %all-to-all-start.4) | async-done | bytes 524320 | tf_op jit(solution)/shard_map/all_to_all | solution.py:489
  148.0 0.1 reduce_sum.35
  148.1 0.9 broadcast_in_dim.8
  149.0 3.5 %all-to-all-start.5 = ((bf16[8,256,128]{2,1,0:T(8,128)(2,1)}), bf16[8,256,128]{2,1,0:T(8,128)(2,1)S(1)}, u32[]{:S(2)}, u32[]{:S(2)}) async-start(bf16[8,256,128]{2,1,0:T(8,128)(2,1)} %broadcast_in_dim.8), calls=%async_computation.5 | async-start | bytes 1048576 | tf_op jit(solution)/shard_map/all_to_all | solution.py:489
  152.5 7.3 %grad_decoder_2.1 = bf16[36,512,256]{2,1,0:T(8,128)(2,1)} custom-call(bf16[8,512,512]{2,1,0:T(8,128)(2,1)} %get-tuple-element.25.refs_0_, bf16[4,512,256]{2,1,0:T(8,128)(2,1)} %bitcast.7, bf16[4,512,256]{2,1,0:T(8,128)(2,1)} %copy-done.1, bf16[36,512,256]{2,1,0:T(8,128)(2,1)} %grad_decoder_0.1.refs_3_), custom_call_target="tpu_custom_call", output_to_operand_aliasing={{}: (3, {})} | custom-call | flops 2818572288 | bytes 5505024 | tf_op jit(solution)/shard_map/grad_decoder_2/pallas_call | solution.py:404
  159.8 2.9 %all-to-all-done.5.slots = bf16[8,256,128]{2,1,0:T(8,128)(2,1)S(1)} async-done(((bf16[8,256,128]{2,1,0:T(8,128)(2,1)}), bf16[8,256,128]{2,1,0:T(8,128)(2,1)S(1)}, u32[]{:S(2)}, u32[]{:S(2)}) %all-to-all-start.5) | async-done | bytes 524320 | tf_op jit(solution)/shard_map/all_to_all | solution.py:489
  162.7 0.0 copy-start.2
  162.7 0.8 copy-done.2
  163.5 12.6 %grad_encoder.1 = (bf16[8,256,512]{2,1,0:T(8,128)(2,1)}, f32[8,512]{1,0:T(8,128)}) custom-call(s32[8,512,512]{2,1,0:T(8,128)} %get-tuple-element.20.ranks_in, bf16[8,256,128]{2,1,0:T(8,128)(2,1)} %copy-done.2, bf16[8,256,512]{2,1,0:T(8,128)(2,1)} %get-tuple-element.27.turned_in), custom_call_target="tpu_custom_call" | custom-call | tf_op jit(solution)/shard_map/grad_encoder/pallas_call | solution.py:459
Async XLA Ops:
  13.7 16.6 %all-to-all-start = ((bf16[8,256,128]{2,1,0:T(8,128)(2,1)}), bf16[8,256,128]{2,1,0:T(8,128)(2,1)S(1)}, u32[]{:S(2)}, u32[]{:S(2)}) async-start(bf16[8,256,128]{2,1,0:T(8,128)(2,1)} %get-tuple-element.17), calls=%async_computation | async-start | bytes 1048576 | tf_op jit(solution)/shard_map/all_to_all | solution.py:489
  63.7 4.4 %collective-permute-start = (bf16[4,512,256]{2,1,0:T(8,128)(2,1)}, bf16[4,512,256]{2,1,0:T(8,128)(2,1)S(1)}, u32[]{:S(2)}, u32[]{:S(2)}) collective-permute-start(bf16[4,512,256]{2,1,0:T(8,128)(2,1)} %get-tuple-element.24), channel_id=1, source_target_pairs={{0,1},{1,0},{2,3},{3,2},{4,5},{5,4},{6,7},{7,6},{8,9},{9,8},{10,11... | collective-permute-start | bytes 3145736 | tf_op jit(solution)/shard_map/ppermute | solution.py:485
  71.1 22.8 %all-to-all-start.2 = ((bf16[8,256,256]{2,1,0:T(8,128)(2,1)}), bf16[8,256,256]{2,1,0:T(8,128)(2,1)S(1)}, u32[]{:S(2)}, u32[]{:S(2)}) async-start(bf16[8,256,256]{2,1,0:T(8,128)(2,1)} %bitcast.1), calls=%async_computation.2 | async-start | bytes 2097152 | tf_op jit(solution)/shard_map/all_to_all | solution.py:493
  114.2 4.7 %copy-start = (bf16[8,256,256]{2,1,0:T(8,128)(2,1)}, bf16[8,256,256]{2,1,0:T(8,128)(2,1)S(1)}, u32[]{:S(2)}) copy-start(bf16[8,256,256]{2,1,0:T(8,128)(2,1)S(1)} %all_to_all.31) | copy-start | bytes 3145732
  114.2 4.7 %collective-permute-start.1 = (bf16[4,512,256]{2,1,0:T(8,128)(2,1)S(1)}, bf16[4,512,256]{2,1,0:T(8,128)(2,1)S(1)}, u32[]{:S(2)}, u32[]{:S(2)}) collective-permute-start(bf16[4,512,256]{2,1,0:T(8,128)(2,1)S(1)} %bitcast.4), channel_id=1, source_target_pairs={{0,1},{1,0},{2,3},{3,2},{4,5},{5,4},{6,7},{7,6},{8,9},{9,8},{10,11... | collective-permute-start | bytes 3145736 | tf_op jit(solution)/shard_map/ppermute | solution.py:485
  118.9 1.0 copy-start.1
  134.3 13.7 %all-to-all-start.4 = ((bf16[8,256,128]{2,1,0:T(8,128)(2,1)}), bf16[8,256,128]{2,1,0:T(8,128)(2,1)S(1)}, u32[]{:S(2)}, u32[]{:S(2)}) async-start(bf16[8,256,128]{2,1,0:T(8,128)(2,1)} %grad_act.1), calls=%async_computation.4 | async-start | bytes 1048576 | tf_op jit(solution)/shard_map/all_to_all | solution.py:489
  149.0 13.7 %all-to-all-start.5 = ((bf16[8,256,128]{2,1,0:T(8,128)(2,1)}), bf16[8,256,128]{2,1,0:T(8,128)(2,1)S(1)}, u32[]{:S(2)}, u32[]{:S(2)}) async-start(bf16[8,256,128]{2,1,0:T(8,128)(2,1)} %broadcast_in_dim.8), calls=%async_computation.5 | async-start | bytes 1048576 | tf_op jit(solution)/shard_map/all_to_all | solution.py:489
  162.7 0.8 copy-start.2

commit v3 on v2

--- a/solution.py
+++ b/solution.py
@@ -41,36 +41,13 @@
     return lax.shift_right_logical(x, jnp.full_like(x, by) if isinstance(by, int) else by)
 
 
-def slot_columns(table):
-    lane = lanes(table.shape[0])
-    base = lane & 64
-    r = lane & 63
-    at = jnp.zeros_like(r)
-    entry = take(table, base)
-    for step in (16, 8, 4, 2, 1):
-        found = take(table, base + at + step)
-        good = right(found, 16) <= r
-        at = jnp.where(good, at + step, at)
-        entry = jnp.where(good, found, entry)
-    k = r - right(entry, 16)
-    left = entry & 0xFFFF
-    spot = jnp.zeros_like(r)
-    for step in (8, 4, 2, 1):
-        low = lax.population_count(left & ((1 << step) - 1))
-        good = k >= low
-        k = jnp.where(good, k - low, k)
-        left = jnp.where(good, right(left, step), left)
-        spot = jnp.where(good, spot + step, spot)
-    return at * 16 + spot
-
-
 def pack(dense, columns_at, write):
     lane = lanes(ROWS)
 
     @pl.loop(0, HALF // ROWS)
     def _(block):
         row = pl.multiple_of(block * ROWS, ROWS)
-        columns = columns_at(row)
+        columns = columns_at(row) & (FW - 1)
         within = columns & 127
         chunk_of = right(columns, 7)
         packed = None
@@ -96,37 +73,22 @@
                 dense[place] = value.astype(BF)
 
 
-def encode_kernel(active, acts, encoder, bias, table_out, columns_out, slots_out, rows, dense):
+def unpack_next(ranks, slots, dense, layer, part, parts):
+    places = [(half, chunk) for half in range(2) for chunk in range(FW // 128)]
+    count = len(places)
+    for half, chunk in places[count * part // parts : count * (part + 1) // parts]:
+        place = (layer, pl.ds(half * HALF, HALF), pl.ds(chunk * 128, 128))
+        rank = ranks[place]
+        value = jnp.where(rank >= 0, take(slots[layer].astype(F32), rank & 127), 0.0)
+        dense[place] = value.astype(BF)
+
+
+def encode_kernel(active, acts, encoder, bias, columns_out, slots_out, rows, dense):
     layer = pl.program_id(0)
     rel = active[0] - lax.axis_index("lat") * FW
-    high = lax.shift_right_arithmetic(rel, jnp.full_like(rel, 5))
-    bits = lax.shift_left(jnp.full_like(rel, 1), rel & 31)
-
-    @pl.when(layer == 0)
-    def _():
-        rows[...] = jnp.zeros_like(rows)
-
-    before = jnp.zeros((1, T), I32)
-    for word in range(16):
-        marked = jnp.where(high == word, bits, 0)
-        folded = marked[0:8]
-        for k in range(8, 64, 8):
-            folded = folded | marked[k : k + 8]
-        both = jnp.sum(folded, axis=0, keepdims=True)
-        for part in range(2):
-            piece = both & 0xFFFF if part == 0 else right(both, 16)
-            entry = piece | lax.shift_left(before, jnp.full_like(before, 16))
-            before = before + lax.population_count(piece)
-            for half in range(2):
-                at = 64 * half + 2 * word + part
-                rows[at : at + 1, :] = entry[:, half * HALF : (half + 1) * HALF]
-    table_out[0] = rows[...].T
-
-    @pl.loop(0, HALF // ROWS)
-    def _(block):
-        at = (0, pl.ds(pl.multiple_of(block * ROWS, ROWS), ROWS), slice(None))
-        columns_out[at] = slot_columns(table_out[at])
-
+    rows[0:64, :] = rel[:, :HALF]
+    rows[64:128, :] = rel[:, HALF:]
+    columns_out[0] = rows[...].T
     added = jnp.where(lax.axis_index("layer") == 0, 1.0, 0.0).astype(F32)
     value = jnp.dot(acts[0], encoder[0], preferred_element_type=F32)
     dense[...] = value + bias[pl.ds(layer, 1), :] * added
@@ -150,9 +112,8 @@
         encode_kernel,
         grid=(LAYERS,),
         in_specs=[one(64, T), one(T, DW), one(DW, FW), whole(LAYERS, FW)],
-        out_specs=[one(HALF, 128), one(HALF, 128), one(HALF, 128)],
+        out_specs=[one(HALF, 128), one(HALF, 128)],
         out_shape=[
-            jax.ShapeDtypeStruct((LAYERS, HALF, 128), I32),
             jax.ShapeDtypeStruct((LAYERS, HALF, 128), I32),
             jax.ShapeDtypeStruct((LAYERS, HALF, 128), BF),
         ],
@@ -162,54 +123,126 @@
     )(active_t, activations, encoder, bias)
 
 
-def ranks_kernel(table, acts, ranks_out, turned_out, ranks, turned, sent):
+def ranks_kernel(active, columns, ranks_out, order_out, rows, table, ranks, sent):
     lane = lanes(ROWS)
     bit = lane & 15
     below = lax.shift_left(jnp.full_like(bit, 1), bit) - 1
+    own = lax.axis_index("layer")
+    first = lax.axis_index("lat") * FW
+    rows[...] = jnp.zeros_like(rows)
+
+    def send(layer):
+        return pltpu.make_async_copy(ranks.at[layer], ranks_out.at[layer], sent.at[layer])
 
     @pl.loop(0, LAYERS)
     def _(layer):
-        turned[layer] = acts[layer].T
-
-        @pl.loop(0, HALF // ROWS)
-        def _(block):
-            row = pl.multiple_of(block * ROWS, ROWS)
-            entries = table[layer, pl.ds(row, ROWS), :]
-            for half in range(2):
-                for chunk in range(FW // 128):
-                    entry = take(entries, 64 * half + 8 * chunk + right(lane, 4))
-                    rank = right(entry, 16) + lax.population_count(entry & below) + 64 * half
-                    hit = (right(entry, bit) & 1) == 1
-                    place = (layer, pl.ds(row + half * HALF, ROWS), pl.ds(chunk * 128, 128))
-                    ranks[place] = jnp.where(hit, rank, -1)
-
-        pltpu.make_async_copy(ranks.at[layer], ranks_out.at[layer], sent.at[layer]).start()
-        pltpu.make_async_copy(turned.at[layer], turned_out.at[layer], sent.at[LAYERS + layer]).start()
-
-    @pl.loop(0, LAYERS)
-    def _(layer):
-        pltpu.make_async_copy(ranks.at[layer], ranks_out.at[layer], sent.at[layer]).wait()
-        pltpu.make_async_copy(turned.at[layer], turned_out.at[layer], sent.at[LAYERS + layer]).wait()
-
-
-def ranks_of(table, activations):
+        rel = active[layer] - first
+        high = lax.shift_right_arithmetic(rel, jnp.full_like(rel, 5))
+        bits = lax.shift_left(jnp.full_like(rel, 1), rel & 31)
+        before = jnp.zeros((1, T), I32)
+        for word in range(16):
+            marked = jnp.where(high == word, bits, 0)
+            folded = marked[0:8]
+            for k in range(8, 64, 8):
+                folded = folded | marked[k : k + 8]
+            both = jnp.sum(folded, axis=0, keepdims=True)
+            for part in range(2):
+                piece = both & 0xFFFF if part == 0 else right(both, 16)
+                entry = piece | lax.shift_left(before, jnp.full_like(before, 16))
+                before = before + lax.population_count(piece)
+                for half in range(2):
+                    at = 64 * half + 2 * word + part
+                    rows[at : at + 1, :] = entry[:, half * HALF : (half + 1) * HALF]
+        entries = rows[...].T
+
+        @pl.when(layer == own)
+        def _():
+            table[...] = entries
+
+        for half in range(2):
+            for chunk in range(FW // 128):
+                entry = take(entries, 64 * half + 8 * chunk + right(lane, 4))
+                rank = right(entry, 16) + lax.population_count(entry & below) + 64 * half
+                hit = (right(entry, bit) & 1) == 1
+                place = (layer, pl.ds(half * HALF, HALF), pl.ds(chunk * 128, 128))
+                ranks[place] = jnp.where(hit, rank, -1)
+        send(layer).start()
+
+    column = columns[own]
+    held = (column >= 0) & (column < FW)
+    column = column & (FW - 1)
+    entry = take(table[...], (lane & 64) + right(column, 4))
+    under = lax.shift_left(jnp.full_like(column, 1), column & 15) - 1
+    rank = right(entry, 16) + lax.population_count(entry & under)
+    turned = jnp.where(held, rank, -1).T
+    slot = lax.broadcasted_iota(I32, (64, HALF), 0)
+    for half in range(2):
+        mine = turned[64 * half : 64 * half + 64]
+        for r in range(64):
+            at = 64 * half + r
+            rows[at : at + 1, :] = 64 * half + jnp.sum(
+                jnp.where(mine == r, slot, 0), axis=0, keepdims=True
+            )
+    order_out[...] = rows[...].T
+    each(LAYERS, send, "wait")
+
+
+def ranks_of(active_t, columns):
     return pl.pallas_call(
         ranks_kernel,
         in_specs=[HELD, HELD],
-        out_specs=[ANY, ANY],
+        out_specs=[ANY, HELD],
         out_shape=[
             jax.ShapeDtypeStruct((LAYERS, T, FW), I32),
-            jax.ShapeDtypeStruct((LAYERS, DW, T), BF),
+            jax.ShapeDtypeStruct((HALF, 128), I32),
         ],
         scratch_shapes=[
+            pltpu.VMEM((128, HALF), I32),
+            pltpu.VMEM((HALF, 128), I32),
             pltpu.VMEM((LAYERS, T, FW), I32),
-            pltpu.VMEM((LAYERS, DW, T), BF),
-            pltpu.SemaphoreType.DMA((2 * LAYERS,)),
-        ],
-        compiler_params=params(),
-        cost_estimate=pl.CostEstimate(flops=4 * 10**9, transcendentals=0, bytes_accessed=12 * 2**20),
+            pltpu.SemaphoreType.DMA((LAYERS,)),
+        ],
+        compiler_params=params(),
+        cost_estimate=pl.CostEstimate(flops=5 * 10**9, transcendentals=0, bytes_accessed=10 * 2**20),
         name="ranks",
-    )(table, activations)
+    )(active_t, columns)
+
+
+def turn_kernel(acts, out):
+    for layer in range(LAYERS):
+        out[layer] = acts[layer].T
+
+
+def turn(activations):
+    return pl.pallas_call(
+        turn_kernel,
+        in_specs=[HELD],
+        out_specs=HELD,
+        out_shape=jax.ShapeDtypeStruct((LAYERS, DW, T), BF),
+        compiler_params=params(),
+        cost_estimate=pl.CostEstimate(flops=10**9, transcendentals=0, bytes_accessed=4 * 2**20),
+        name="turn",
+    )(activations)
+
+
+def settle_kernel(parts, order, out):
+    own = parts[0].astype(F32)
+    for i in range(1, LAYERS):
+        own = own + parts[i].astype(F32)
+    own = take(own, order[...]).astype(BF)
+    for i in range(LAYERS):
+        out[i] = own
+
+
+def settle(parts, order):
+    return pl.pallas_call(
+        settle_kernel,
+        in_specs=[HELD, HELD],
+        out_specs=HELD,
+        out_shape=jax.ShapeDtypeStruct((LAYERS, HALF, 128), BF),
+        compiler_params=params(),
+        name="settle",
+    )(parts, order)
 
 
 def each(count, copy, act):
@@ -248,28 +281,30 @@
         def _(target):
             load_pair(first_pair(source) + target - source).start()
 
-    total[...] = jnp.zeros_like(total)
-
-    @pl.loop(0, LAYERS)
-    def _(source):
-        load_ranks(source).wait()
-        unpack(ranks.at[source], slots.at[source], latent.at[source])
+    load_ranks(0).wait()
+    unpack(ranks.at[0], slots.at[0], latent.at[0])
+    for source in range(LAYERS):
+        if source + 1 < LAYERS:
+            load_ranks(source + 1).wait()
+        for target in range(source, LAYERS):
+            load_pair(first_pair(source) + target - source).wait()
         send_latent(source).start()
-
-        @pl.loop(source, LAYERS)
-        def _(target):
+        count = LAYERS - source
+        for i, target in enumerate(range(source, LAYERS)):
             p = first_pair(source) + target - source
-            load_pair(p).wait()
-            total[target] += jnp.dot(latent[source], held[p], preferred_element_type=F32)
+            part = jnp.dot(latent[source], held[p], preferred_element_type=F32)
+            total[target] = part if source == 0 else total[target] + part
+            if source + 1 < LAYERS:
+                unpack_next(ranks, slots, latent, source + 1, i, count)
 
         spot = source % 4
 
         @pl.when(source // 4 == core)
-        def _():
+        def _(spot=spot):
             send_own(spot).start()
 
         @pl.when(source // 4 != core)
-        def _():
+        def _(spot=spot, source=source):
             stage[spot] = total[source].astype(BF)
             send_other(spot).start()
 
@@ -441,16 +476,18 @@
         load_ranks(layer).start()
         load_turned(layer).start()
 
-    @pl.loop(0, LAYERS)
-    def _(layer):
-        load_ranks(layer).wait()
-        unpack(ranks.at[layer], slots.at[layer], dense.at[layer])
-
+    load_ranks(0).wait()
+    unpack(ranks.at[0], slots.at[0], dense.at[0])
     for layer in range(LAYERS):
         load_turned(layer).wait()
+        if layer + 1 < LAYERS:
+            load_ranks(layer + 1).wait()
+            unpack_next(ranks, slots, dense, layer + 1, 0, 1)
         grad[layer] = jnp.dot(turned[layer], dense[layer], preferred_element_type=F32).astype(BF)
+        bias_out[layer : layer + 1, :] = jnp.dot(
+            jnp.ones((16, T), BF), dense[layer], preferred_element_type=F32
+        )[0:1]
         send(layer).start()
-        bias_out[pl.ds(layer, 1), :] = jnp.sum(dense[layer].astype(F32), axis=0, keepdims=True)
 
     each(LAYERS, send, "wait")
 
@@ -493,30 +530,28 @@
     return lax.all_to_all(x, "lat", 0, 0, axis_index_groups=CHIPS, tiled=True)
 
 
-def sum_slots(slots, beside):
-    own = jnp.sum(over_layer(slots).astype(F32), axis=0).astype(BF)
-    own, beside = lax.optimization_barrier((own, beside))
-    return over_layer(jnp.broadcast_to(own[None], slots.shape)), beside
-
-
 def on_device(activations, targets, encoder, bias, decoder, active):
     lat = lax.axis_index("lat")
     first_row = ((lat % 2) * 8 + lat // 2) * 256
-    table, columns, partial = encode(jnp.swapaxes(active, 1, 2), activations, encoder, bias)
-    ranks, turned = ranks_of(table, activations)
-    latent_slots, ranks = sum_slots(partial, ranks)
-    latent, own, send = rebuild(ranks, latent_slots, decoder)
+    active_t = jnp.swapaxes(active, 1, 2)
+    columns, partial = encode(active_t, activations, encoder, bias)
+    ranks, order = ranks_of(active_t, columns)
+    settled = settle(over_layer(partial), order)
+    settled, late = lax.optimization_barrier((settled, activations))
+    turned = turn(late)
+    latent, own, send = rebuild(ranks, over_layer(settled), decoder)
     half = (own + swap_cores(send).astype(F32)).astype(BF).reshape(8, 256, DW)
     total = jnp.sum(over_chips(half).astype(F32), axis=0)
     wanted = lax.dynamic_slice_in_dim(targets.reshape(LAYERS * T, DW), first_row, 256)
     error = (total - wanted.astype(F32)).astype(BF)
     mine = over_chips(jnp.broadcast_to(error[None], (8, 256, DW))).reshape(4, T, DW)
     other = swap_cores(mine)
-    grad_slots = grad_act(columns, mine, other, decoder)
-    grad_decoder = grad_decoder_part(latent, mine, other, 0, 2)
-    grad_slots, grad_decoder = sum_slots(grad_slots, grad_decoder)
-    grad_decoder = grad_decoder_part(latent, mine, other, 2, LAYERS, grad_decoder)
-    grad_encoder, grad_bias = grad_encoder_of(ranks, grad_slots, turned)
+    parts = over_layer(grad_act(columns, mine, other, decoder))
+    grad_decoder = grad_decoder_part(latent, mine, other, 0, 3)
+    parts, grad_decoder = lax.optimization_barrier((parts, grad_decoder))
+    settled = over_layer(settle(parts, order))
+    grad_decoder = grad_decoder_part(latent, mine, other, 3, LAYERS, grad_decoder)
+    grad_encoder, grad_bias = grad_encoder_of(ranks, settled, turned)
     return (grad_encoder, grad_bias, grad_decoder)
 
 

time: 177 us -> 169 us (0.955)
  waiting for transfers between devices: 31.6 us -> 24.6 us
  Pallas kernels: 80.4 us -> 76 us
  blocking collectives: 31.4 us -> 33.4 us
    pallas_call x1 -> x4, Pallas kernels: 6.67 us -> 18.5 us  [the longest x1 10.8 us: ranks_of(): pl.pallas_call(ranks_kernel, in_specs=[HELD, HELD], out_specs=[ANY, HELD]...]
    pallas_call x1, Pallas kernels: 21 us -> 11.9 us  [rebuild(): pl.pallas_call(rebuild_kernel, in_specs=[ANY, HELD, ANY], out_specs=[ANY,...]
    all_to_all x3, waiting for transfers between devices: 11.1 us -> 4.08 us  [over_layer(): return lax.all_to_all(x, 'layer', 0, 0, tiled=True)]
    pallas_call x1, Pallas kernels: 13.1 us -> 8.01 us  [encode(): pl.pallas_call(encode_kernel, grid=(LAYERS,), in_specs=[one(64, T), one(T...]
    all_to_all x1, blocking collectives: 12.2 us -> 14.2 us  [over_layer(): return lax.all_to_all(x, 'layer', 0, 0, tiled=True)]
    pallas_call x1, Pallas kernels: 12.6 us -> 10.6 us  [grad_encoder_of(): pl.pallas_call(grad_encoder_kernel, in_specs=[ANY, HELD, ANY], out_specs=...]
  transfers between devices with their start and end apart: 6 -> 6, of which waited for: 6 -> 5; matrix products, arithmetic and copies ran while one was open for 0% -> 0% of each run, Pallas kernels for 11% -> 16%
where the time goes in v3:
time: 169 us; the launch traced here: 168 us
  Pallas kernels  76 us (45%)
  blocking collectives  33.4 us (20%)
  starting transfers between devices  25.1 us (15%)
  waiting for transfers between devices  24.6 us (15%)
  other arithmetic  4.07 us (2%)
  local copies, waits for them, and re-layouts  3.51 us (2%)
    all_to_all x1, blocking collectives, over_chips(): return lax.all_to_all(x, 'lat', 0, 0, axis_index_groups=CHIPS, tiled=True)  19.2 us
    all_to_all x1, waiting for transfers between devices, over_chips(): return lax.all_to_all(x, 'lat', 0, 0, axis_index_groups=CHIPS, tiled=True)  15.8 us
    pallas_call x1, Pallas kernels, grad_act(): pl.pallas_call(grad_act_kernel, in_specs=[HELD, ANY, ANY, ANY], out_specs...  14.4 us
    all_to_all x1, blocking collectives, over_layer(): return lax.all_to_all(x, 'layer', 0, 0, tiled=True)  14.2 us
    all_to_all x3, starting transfers between devices, over_layer(): return lax.all_to_all(x, 'layer', 0, 0, tiled=True)  13.6 us
    pallas_call x2, Pallas kernels, grad_decoder_part(): pl.pallas_call(kernel, in_specs=[ANY] * len(operands), out_specs=ANY, out...  12.5 us
    pallas_call x1, Pallas kernels, rebuild(): pl.pallas_call(rebuild_kernel, in_specs=[ANY, HELD, ANY], out_specs=[ANY,...  11.9 us
    pallas_call x1, Pallas kernels, ranks_of(): pl.pallas_call(ranks_kernel, in_specs=[HELD, HELD], out_specs=[ANY, HELD]...  10.8 us
  transfers between devices with their start and end apart: 6, of which 5 were waited for; matrix products, arithmetic and copies ran while one was open for 0% of the time, Pallas kernels for 16%

profile of v3, /device:TPU:1, one launch (start us, length us, event | category | flops | bytes accessed | tf_op | source)
XLA Modules:
  0.0 167.6 jit_solution(1749466625959049768)
XLA Ops:
  0.6 8.0 %encode.1 = (s32[8,256,128]{2,1,0:T(8,128)}, bf16[8,256,128]{2,1,0:T(8,128)(2,1)}) custom-call(s32[8,64,512]{2,1,0:T(8,128)} %bitcast.8, bf16[8,512,256]{2,1,0:T(8,128)(2,1)} %acts.2, bf16[8,256,512]{2,1,0:T(8,128)(2,1)} %encoder.1, f32[8,512]{1,0:T(8,128)} %bias.1), custom_call_target="tpu_custom_call" | custom-call | tf_op jit(solution)/shard_map/encode/pallas_call | solution.py:111
  8.6 6.4 %all-to-all-start = ((bf16[8,256,128]{2,1,0:T(8,128)(2,1)}), bf16[8,256,128]{2,1,0:T(8,128)(2,1)S(1)}, u32[]{:S(2)}, u32[]{:S(2)}) async-start(bf16[8,256,128]{2,1,0:T(8,128)(2,1)} %get-tuple-element.18), calls=%async_computation | async-start | bytes 1048576 | tf_op jit(solution)/shard_map/all_to_all | solution.py:526
  15.0 10.8 %ranks.1 = (s32[8,512,512]{2,1,0:T(8,128)}, s32[256,128]{1,0:T(8,128)}) custom-call(s32[8,64,512]{2,1,0:T(8,128)} %bitcast.9, s32[8,256,128]{2,1,0:T(8,128)} %get-tuple-element.16.columns), custom_call_target="tpu_custom_call" | custom-call | flops 5000000000 | bytes 10485760 | tf_op jit(solution)/shard_map/ranks/pallas_call | solution.py:191
  25.8 0.0 all-to-all-done.parts
  25.9 0.0 copy-start.2
  25.9 0.8 copy-done.2
  26.7 2.1 %settle.2 = bf16[8,256,128]{2,1,0:T(8,128)(2,1)} custom-call(bf16[8,256,128]{2,1,0:T(8,128)(2,1)} %copy-done.2, s32[256,128]{1,0:T(8,128)} %get-tuple-element.19.order), custom_call_target="tpu_custom_call" | custom-call | tf_op jit(solution)/shard_map/settle/pallas_call | solution.py:238
  28.7 14.2 %all_to_all.30.slots = bf16[8,256,128]{2,1,0:T(8,128)(2,1)} all-to-all(bf16[8,256,128]{2,1,0:T(8,128)(2,1)} %settle.2), channel_id=1, replica_groups=mesh['layer'=8,'lat'=16] {'layer'}, dimensions={0} | all-to-all | bytes 1048576 | tf_op jit(solution)/shard_map/all_to_all | solution.py:526
  42.9 11.9 %rebuild.1 = (bf16[8,512,512]{2,1,0:T(8,128)(2,1)}, f32[4,512,256]{2,1,0:T(8,128)}, bf16[4,512,256]{2,1,0:T(8,128)(2,1)}) custom-call(s32[8,512,512]{2,1,0:T(8,128)} %get-tuple-element.17.ranks_in, bf16[8,256,128]{2,1,0:T(8,128)(2,1)} %all_to_all.30.slots, bf16[36,512,256]{2,1,0:T(8,128)(2,1)} %decoder.3), custom_call_target="tpu_custom_call" | custom-call | tf_op jit(solution)/shard_map/rebuild/pallas_call | solution.py:317
  54.8 2.1 %collective-permute-start = (bf16[4,512,256]{2,1,0:T(8,128)(2,1)}, bf16[4,512,256]{2,1,0:T(8,128)(2,1)S(1)}, u32[]{:S(2)}, u32[]{:S(2)}) collective-permute-start(bf16[4,512,256]{2,1,0:T(8,128)(2,1)} %get-tuple-element.22), channel_id=1, source_target_pairs={{0,1},{1,0},{2,3},{3,2},{4,5},{5,4},{6,7},{7,6},{8,9},{9,8},{10,11... | collective-permute-start | bytes 3145736 | tf_op jit(solution)/shard_map/ppermute | solution.py:522
  56.9 2.5 %collective-permute-done = bf16[4,512,256]{2,1,0:T(8,128)(2,1)S(1)} collective-permute-done((bf16[4,512,256]{2,1,0:T(8,128)(2,1)}, bf16[4,512,256]{2,1,0:T(8,128)(2,1)S(1)}, u32[]{:S(2)}, u32[]{:S(2)}) %collective-permute-start) | collective-permute-done | bytes 1048608 | tf_op jit(solution)/shard_map/ppermute | solution.py:522
  59.4 3.0 %add_convert_fusion = bf16[4,512,256]{2,1,0:T(8,128)(2,1)} fusion(f32[4,512,256]{2,1,0:T(8,128)} %get-tuple-element.21, bf16[4,512,256]{2,1,0:T(8,128)(2,1)S(1)} %collective-permute-done), kind=kLoop, calls=%fused_computation.1 | loop fusion | flops 1572864 | bytes 4194304 | tf_op jit(solution)/shard_map/convert_element_type | solution.py:543
  62.4 7.1 %all-to-all-start.2 = ((bf16[8,256,256]{2,1,0:T(8,128)(2,1)}), bf16[8,256,256]{2,1,0:T(8,128)(2,1)S(1)}, u32[]{:S(2)}, u32[]{:S(2)}) async-start(bf16[8,256,256]{2,1,0:T(8,128)(2,1)} %bitcast.1), calls=%async_computation.2 | async-start | bytes 2097152 | tf_op jit(solution)/shard_map/all_to_all | solution.py:530
  69.4 15.8 %all-to-all-done.2 = bf16[8,256,256]{2,1,0:T(8,128)(2,1)S(1)} async-done(((bf16[8,256,256]{2,1,0:T(8,128)(2,1)}), bf16[8,256,256]{2,1,0:T(8,128)(2,1)S(1)}, u32[]{:S(2)}, u32[]{:S(2)}) %all-to-all-start.2) | async-done | bytes 1048608 | tf_op jit(solution)/shard_map/all_to_all | solution.py:530
  85.2 0.1 convert_reduce_fusion
  85.3 0.9 subtract_convert_fusion
  86.3 0.1 broadcast_in_dim.2
  86.4 19.2 %all_to_all.31 = bf16[8,256,256]{2,1,0:T(8,128)(2,1)S(1)} all-to-all(bf16[8,256,256]{2,1,0:T(8,128)(2,1)S(1)} %broadcast_in_dim.2), channel_id=1, replica_groups={{0,2,4,6,8,10,12,14},{1,3,5,7,9,11,13,15},{16,18,20,22,24,26,28,30},{17..., dimensions={0} | all-to-all | bytes 2097152 | tf_op jit(solution)/shard_map/all_to_all | solution.py:530
  105.5 0.0 copy-start
  105.5 2.4 %collective-permute-start.1 = (bf16[4,512,256]{2,1,0:T(8,128)(2,1)S(1)}, bf16[4,512,256]{2,1,0:T(8,128)(2,1)S(1)}, u32[]{:S(2)}, u32[]{:S(2)}) collective-permute-start(bf16[4,512,256]{2,1,0:T(8,128)(2,1)S(1)} %bitcast.4), channel_id=1, source_target_pairs={{0,1},{1,0},{2,3},{3,2},{4,5},{5,4},{6,7},{7,6},{8,9},{9,8},{10,11... | collective-permute-start | bytes 3145736 | tf_op jit(solution)/shard_map/ppermute | solution.py:522
  108.0 2.3 %collective-permute-done.1.other.refs_2_ = bf16[4,512,256]{2,1,0:T(8,128)(2,1)S(1)} collective-permute-done((bf16[4,512,256]{2,1,0:T(8,128)(2,1)S(1)}, bf16[4,512,256]{2,1,0:T(8,128)(2,1)S(1)}, u32[]{:S(2)}, u32[]{:S(2)}) %collective-permute-start.1) | collective-permute-done | bytes 1048608 | tf_op jit(solution)/shard_map/ppermute | solution.py:522
  110.3 0.0 copy-done
  110.3 0.0 copy-start.1
  110.3 1.0 copy-done.1
  111.2 14.4 %grad_act.1 = bf16[8,256,128]{2,1,0:T(8,128)(2,1)} custom-call(s32[8,256,128]{2,1,0:T(8,128)} %get-tuple-element.16.columns, bf16[4,512,256]{2,1,0:T(8,128)(2,1)} %bitcast.5, bf16[4,512,256]{2,1,0:T(8,128)(2,1)} %copy-done.1, bf16[36,512,256]{2,1,0:T(8,128)(2,1)} %decoder.3), custom_call_target="tpu_custom_call" | custom-call | tf_op jit(solution)/shard_map/grad_act/pallas_call | solution.py:384
  125.7 3.5 %all-to-all-start.4 = ((bf16[8,256,128]{2,1,0:T(8,128)(2,1)}), bf16[8,256,128]{2,1,0:T(8,128)(2,1)S(1)}, u32[]{:S(2)}, u32[]{:S(2)}) async-start(bf16[8,256,128]{2,1,0:T(8,128)(2,1)} %grad_act.1), calls=%async_computation.4 | async-start | bytes 1048576 | tf_op jit(solution)/shard_map/all_to_all | solution.py:526
  129.2 6.6 %grad_decoder_0.1.refs_3_ = bf16[36,512,256]{2,1,0:T(8,128)(2,1)} custom-call(bf16[8,512,512]{2,1,0:T(8,128)(2,1)} %get-tuple-element.23.refs_0_, bf16[4,512,256]{2,1,0:T(8,128)(2,1)} %bitcast.6, bf16[4,512,256]{2,1,0:T(8,128)(2,1)} %copy-done.1), custom_call_target="tpu_custom_call" | custom-call | flops 2818572288 | bytes 5505024 | tf_op jit(solution)/shard_map/grad_decoder_0/pallas_call | solution.py:439
  135.8 3.6 %all-to-all-done.4.parts = bf16[8,256,128]{2,1,0:T(8,128)(2,1)S(1)} async-done(((bf16[8,256,128]{2,1,0:T(8,128)(2,1)}), bf16[8,256,128]{2,1,0:T(8,128)(2,1)S(1)}, u32[]{:S(2)}, u32[]{:S(2)}) %all-to-all-start.4) | async-done | bytes 524320 | tf_op jit(solution)/shard_map/all_to_all | solution.py:526
  139.4 0.0 copy-start.3
  139.4 0.8 copy-done.3
  140.2 2.0 %settle.3 = bf16[8,256,128]{2,1,0:T(8,128)(2,1)} custom-call(bf16[8,256,128]{2,1,0:T(8,128)(2,1)} %copy-done.3, s32[256,128]{1,0:T(8,128)} %get-tuple-element.19.order), custom_call_target="tpu_custom_call" | custom-call | tf_op jit(solution)/shard_map/settle/pallas_call | solution.py:238
  142.3 3.7 %all-to-all-start.5 = ((bf16[8,256,128]{2,1,0:T(8,128)(2,1)}), bf16[8,256,128]{2,1,0:T(8,128)(2,1)S(1)}, u32[]{:S(2)}, u32[]{:S(2)}) async-start(bf16[8,256,128]{2,1,0:T(8,128)(2,1)} %settle.3), calls=%async_computation.5 | async-start | bytes 1048576 | tf_op jit(solution)/shard_map/all_to_all | solution.py:526
  146.0 3.5 %turn.1.turned_in = bf16[8,256,512]{2,1,0:T(8,128)(2,1)} custom-call(bf16[8,512,256]{2,1,0:T(8,128)(2,1)} %acts.2), custom_call_target="tpu_custom_call" | custom-call | flops 1000000000 | bytes 4194304 | tf_op jit(solution)/shard_map/turn/pallas_call | solution.py:217
  149.5 6.0 %grad_decoder_3.1 = bf16[36,512,256]{2,1,0:T(8,128)(2,1)} custom-call(bf16[8,512,512]{2,1,0:T(8,128)(2,1)} %get-tuple-element.23.refs_0_, bf16[4,512,256]{2,1,0:T(8,128)(2,1)} %bitcast.7, bf16[4,512,256]{2,1,0:T(8,128)(2,1)} %copy-done.1, bf16[36,512,256]{2,1,0:T(8,128)(2,1)} %grad_decoder_0.1.refs_3_), custom_call_target="tpu_custom_call", output_to_operand_aliasing={{}: (3, {})} | custom-call | flops 2013265920 | bytes 3932160 | tf_op jit(solution)/shard_map/grad_decoder_3/pallas_call | solution.py:439
  155.5 0.4 all-to-all-done.5.slots
  156.0 0.0 copy-start.4
  156.0 0.8 copy-done.4
  156.8 10.6 %grad_encoder.1 = (bf16[8,256,512]{2,1,0:T(8,128)(2,1)}, f32[8,512]{1,0:T(8,128)}) custom-call(s32[8,512,512]{2,1,0:T(8,128)} %get-tuple-element.17.ranks_in, bf16[8,256,128]{2,1,0:T(8,128)(2,1)} %copy-done.4, bf16[8,256,512]{2,1,0:T(8,128)(2,1)} %turn.1.turned_in), custom_call_target="tpu_custom_call" | custom-call | tf_op jit(solution)/shard_map/grad_encoder/pallas_call | solution.py:496
Async XLA Ops:
  8.6 17.2 %all-to-all-start = ((bf16[8,256,128]{2,1,0:T(8,128)(2,1)}), bf16[8,256,128]{2,1,0:T(8,128)(2,1)S(1)}, u32[]{:S(2)}, u32[]{:S(2)}) async-start(bf16[8,256,128]{2,1,0:T(8,128)(2,1)} %get-tuple-element.18), calls=%async_computation | async-start | bytes 1048576 | tf_op jit(solution)/shard_map/all_to_all | solution.py:526
  25.9 0.8 copy-start.2
  54.8 4.6 %collective-permute-start = (bf16[4,512,256]{2,1,0:T(8,128)(2,1)}, bf16[4,512,256]{2,1,0:T(8,128)(2,1)S(1)}, u32[]{:S(2)}, u32[]{:S(2)}) collective-permute-start(bf16[4,512,256]{2,1,0:T(8,128)(2,1)} %get-tuple-element.22), channel_id=1, source_target_pairs={{0,1},{1,0},{2,3},{3,2},{4,5},{5,4},{6,7},{7,6},{8,9},{9,8},{10,11... | collective-permute-start | bytes 3145736 | tf_op jit(solution)/shard_map/ppermute | solution.py:522
  62.4 22.8 %all-to-all-start.2 = ((bf16[8,256,256]{2,1,0:T(8,128)(2,1)}), bf16[8,256,256]{2,1,0:T(8,128)(2,1)S(1)}, u32[]{:S(2)}, u32[]{:S(2)}) async-start(bf16[8,256,256]{2,1,0:T(8,128)(2,1)} %bitcast.1), calls=%async_computation.2 | async-start | bytes 2097152 | tf_op jit(solution)/shard_map/all_to_all | solution.py:530
  105.5 4.7 %copy-start = (bf16[8,256,256]{2,1,0:T(8,128)(2,1)}, bf16[8,256,256]{2,1,0:T(8,128)(2,1)S(1)}, u32[]{:S(2)}) copy-start(bf16[8,256,256]{2,1,0:T(8,128)(2,1)S(1)} %all_to_all.31) | copy-start | bytes 3145732
  105.5 4.7 %collective-permute-start.1 = (bf16[4,512,256]{2,1,0:T(8,128)(2,1)S(1)}, bf16[4,512,256]{2,1,0:T(8,128)(2,1)S(1)}, u32[]{:S(2)}, u32[]{:S(2)}) collective-permute-start(bf16[4,512,256]{2,1,0:T(8,128)(2,1)S(1)} %bitcast.4), channel_id=1, source_target_pairs={{0,1},{1,0},{2,3},{3,2},{4,5},{5,4},{6,7},{7,6},{8,9},{9,8},{10,11... | collective-permute-start | bytes 3145736 | tf_op jit(solution)/shard_map/ppermute | solution.py:522
  110.3 1.0 copy-start.1
  125.7 13.7 %all-to-all-start.4 = ((bf16[8,256,128]{2,1,0:T(8,128)(2,1)}), bf16[8,256,128]{2,1,0:T(8,128)(2,1)S(1)}, u32[]{:S(2)}, u32[]{:S(2)}) async-start(bf16[8,256,128]{2,1,0:T(8,128)(2,1)} %grad_act.1), calls=%async_computation.4 | async-start | bytes 1048576 | tf_op jit(solution)/shard_map/all_to_all | solution.py:526
  139.4 0.8 copy-start.3
  142.3 13.7 %all-to-all-start.5 = ((bf16[8,256,128]{2,1,0:T(8,128)(2,1)}), bf16[8,256,128]{2,1,0:T(8,128)(2,1)S(1)}, u32[]{:S(2)}, u32[]{:S(2)}) async-start(bf16[8,256,128]{2,1,0:T(8,128)(2,1)} %settle.3), calls=%async_computation.5 | async-start | bytes 1048576 | tf_op jit(solution)/shard_map/all_to_all | solution.py:526
  156.0 0.8 copy-start.4

commit v4 on v3

--- a/solution.py
+++ b/solution.py
@@ -41,23 +41,26 @@
     return lax.shift_right_logical(x, jnp.full_like(x, by) if isinstance(by, int) else by)
 
 
+def pack_rows(dense, columns, row, write):
+    lane = lanes(ROWS)
+    columns = columns & (FW - 1)
+    within = columns & 127
+    chunk_of = right(columns, 7)
+    packed = None
+    for chunk in range(FW // 128):
+        part = pl.ds(chunk * 128, 128)
+        low = take(dense[pl.ds(row, ROWS), part], within)
+        high = take(dense[pl.ds(row + HALF, ROWS), part], within)
+        picked = jnp.where(lane < 64, low, high)
+        packed = picked if packed is None else jnp.where(chunk_of == chunk, picked, packed)
+    write(row, packed.astype(BF))
+
+
 def pack(dense, columns_at, write):
-    lane = lanes(ROWS)
-
     @pl.loop(0, HALF // ROWS)
     def _(block):
         row = pl.multiple_of(block * ROWS, ROWS)
-        columns = columns_at(row) & (FW - 1)
-        within = columns & 127
-        chunk_of = right(columns, 7)
-        packed = None
-        for chunk in range(FW // 128):
-            part = pl.ds(chunk * 128, 128)
-            low = take(dense[pl.ds(row, ROWS), part], within)
-            high = take(dense[pl.ds(row + HALF, ROWS), part], within)
-            picked = jnp.where(lane < 64, low, high)
-            packed = picked if packed is None else jnp.where(chunk_of == chunk, picked, packed)
-        write(row, packed.astype(BF))
+        pack_rows(dense, columns_at(row), row, write)
 
 
 def unpack(ranks, slots, dense):
@@ -364,20 +367,28 @@
     for load in loads:
         each(4, load, "wait")
 
+    def pack_layer(layer):
+        def write(row, packed):
+            slots_out[layer, pl.ds(row, ROWS), :] = packed
+
+        pack_rows(total.at[layer % 2], columns[layer], 0, write)
+
     for source in range(LAYERS):
         for target in range(source, LAYERS):
-            p = first_pair(source) + target - source
-            load_pair(p).wait()
+            load_pair(first_pair(source) + target - source).wait()
+        summed = None
+        for target in range(source, LAYERS):
             part = lax.dot_general(
-                errors[target], held[p], (((1,), (1,)), ((), ())), preferred_element_type=F32
+                errors[target],
+                held[first_pair(source) + target - source],
+                (((1,), (1,)), ((), ())),
+                preferred_element_type=F32,
             )
-            summed = part if target == source else summed + part
-        total[...] = summed
-
-        def write(row, packed):
-            slots_out[source, pl.ds(row, ROWS), :] = packed
-
-        pack(total, lambda row: columns[source, pl.ds(row, ROWS), :], write)
+            summed = part if summed is None else summed + part
+        total[source % 2] = summed
+        if source > 0:
+            pack_layer(source - 1)
+    pack_layer(LAYERS - 1)
 
 
 def grad_act(columns, mine, other, decoder):
@@ -388,7 +399,7 @@
         out_shape=jax.ShapeDtypeStruct((LAYERS, HALF, 128), BF),
         scratch_shapes=[
             pltpu.VMEM((LAYERS, T, DW), BF),
-            pltpu.VMEM((T, FW), F32),
+            pltpu.VMEM((2, T, FW), F32),
             pltpu.VMEM((PAIRS, FW, DW), BF),
             pltpu.SemaphoreType.DMA((LAYERS,)),
             pltpu.SemaphoreType.DMA((PAIRS,)),

time: 169 us -> 166 us (0.982)
  Pallas kernels: 76 us -> 73 us
    pallas_call x1, Pallas kernels: 14.4 us -> 11.5 us  [grad_act(): pl.pallas_call(grad_act_kernel, in_specs=[HELD, ANY, ANY, ANY], out_specs...]
where the time goes in v4:
time: 166 us; the launch traced here: 165 us
  Pallas kernels  73 us (44%)
  blocking collectives  33.4 us (20%)
  starting transfers between devices  25.1 us (15%)
  waiting for transfers between devices  24.6 us (15%)
  other arithmetic  4.07 us (2%)
  local copies, waits for them, and re-layouts  3.51 us (2%)
    all_to_all x1, blocking collectives, over_chips(): return lax.all_to_all(x, 'lat', 0, 0, axis_index_groups=CHIPS, tiled=True)  19.2 us
    all_to_all x1, waiting for transfers between devices, over_chips(): return lax.all_to_all(x, 'lat', 0, 0, axis_index_groups=CHIPS, tiled=True)  15.8 us
    all_to_all x1, blocking collectives, over_layer(): return lax.all_to_all(x, 'layer', 0, 0, tiled=True)  14.2 us
    all_to_all x3, starting transfers between devices, over_layer(): return lax.all_to_all(x, 'layer', 0, 0, tiled=True)  13.6 us
    pallas_call x2, Pallas kernels, grad_decoder_part(): pl.pallas_call(kernel, in_specs=[ANY] * len(operands), out_specs=ANY, out...  12.5 us
    pallas_call x1, Pallas kernels, rebuild(): pl.pallas_call(rebuild_kernel, in_specs=[ANY, HELD, ANY], out_specs=[ANY,...  11.9 us
    pallas_call x1, Pallas kernels, grad_act(): pl.pallas_call(grad_act_kernel, in_specs=[HELD, ANY, ANY, ANY], out_specs...  11.5 us
    pallas_call x1, Pallas kernels, ranks_of(): pl.pallas_call(ranks_kernel, in_specs=[HELD, HELD], out_specs=[ANY, HELD]...  10.8 us
  transfers between devices with their start and end apart: 6, of which 5 were waited for; matrix products, arithmetic and copies ran while one was open for 0% of the time, Pallas kernels for 16%

profile of v4, /device:TPU:1, one launch (start us, length us, event | category | flops | bytes accessed | tf_op | source)
XLA Modules:
  0.0 164.6 jit_solution(17976255884087359350)
XLA Ops:
  0.6 8.0 %encode.1 = (s32[8,256,128]{2,1,0:T(8,128)}, bf16[8,256,128]{2,1,0:T(8,128)(2,1)}) custom-call(s32[8,64,512]{2,1,0:T(8,128)} %bitcast.8, bf16[8,512,256]{2,1,0:T(8,128)(2,1)} %acts.2, bf16[8,256,512]{2,1,0:T(8,128)(2,1)} %encoder.1, f32[8,512]{1,0:T(8,128)} %bias.1), custom_call_target="tpu_custom_call" | custom-call | tf_op jit(solution)/shard_map/encode/pallas_call | solution.py:114
  8.6 6.4 %all-to-all-start = ((bf16[8,256,128]{2,1,0:T(8,128)(2,1)}), bf16[8,256,128]{2,1,0:T(8,128)(2,1)S(1)}, u32[]{:S(2)}, u32[]{:S(2)}) async-start(bf16[8,256,128]{2,1,0:T(8,128)(2,1)} %get-tuple-element.18), calls=%async_computation | async-start | bytes 1048576 | tf_op jit(solution)/shard_map/all_to_all | solution.py:537
  15.0 10.8 %ranks.1 = (s32[8,512,512]{2,1,0:T(8,128)}, s32[256,128]{1,0:T(8,128)}) custom-call(s32[8,64,512]{2,1,0:T(8,128)} %bitcast.9, s32[8,256,128]{2,1,0:T(8,128)} %get-tuple-element.16.columns), custom_call_target="tpu_custom_call" | custom-call | flops 5000000000 | bytes 10485760 | tf_op jit(solution)/shard_map/ranks/pallas_call | solution.py:194
  25.8 0.0 all-to-all-done.parts
  25.9 0.0 copy-start.2
  25.9 0.8 copy-done.2
  26.7 2.1 %settle.2 = bf16[8,256,128]{2,1,0:T(8,128)(2,1)} custom-call(bf16[8,256,128]{2,1,0:T(8,128)(2,1)} %copy-done.2, s32[256,128]{1,0:T(8,128)} %get-tuple-element.19.order), custom_call_target="tpu_custom_call" | custom-call | tf_op jit(solution)/shard_map/settle/pallas_call | solution.py:241
  28.7 14.2 %all_to_all.30.slots = bf16[8,256,128]{2,1,0:T(8,128)(2,1)} all-to-all(bf16[8,256,128]{2,1,0:T(8,128)(2,1)} %settle.2), channel_id=1, replica_groups=mesh['layer'=8,'lat'=16] {'layer'}, dimensions={0} | all-to-all | bytes 1048576 | tf_op jit(solution)/shard_map/all_to_all | solution.py:537
  42.9 11.9 %rebuild.1 = (bf16[8,512,512]{2,1,0:T(8,128)(2,1)}, f32[4,512,256]{2,1,0:T(8,128)}, bf16[4,512,256]{2,1,0:T(8,128)(2,1)}) custom-call(s32[8,512,512]{2,1,0:T(8,128)} %get-tuple-element.17.ranks_in, bf16[8,256,128]{2,1,0:T(8,128)(2,1)} %all_to_all.30.slots, bf16[36,512,256]{2,1,0:T(8,128)(2,1)} %decoder.3), custom_call_target="tpu_custom_call" | custom-call | tf_op jit(solution)/shard_map/rebuild/pallas_call | solution.py:320
  54.8 2.1 %collective-permute-start = (bf16[4,512,256]{2,1,0:T(8,128)(2,1)}, bf16[4,512,256]{2,1,0:T(8,128)(2,1)S(1)}, u32[]{:S(2)}, u32[]{:S(2)}) collective-permute-start(bf16[4,512,256]{2,1,0:T(8,128)(2,1)} %get-tuple-element.22), channel_id=1, source_target_pairs={{0,1},{1,0},{2,3},{3,2},{4,5},{5,4},{6,7},{7,6},{8,9},{9,8},{10,11... | collective-permute-start | bytes 3145736 | tf_op jit(solution)/shard_map/ppermute | solution.py:533
  56.9 2.5 %collective-permute-done = bf16[4,512,256]{2,1,0:T(8,128)(2,1)S(1)} collective-permute-done((bf16[4,512,256]{2,1,0:T(8,128)(2,1)}, bf16[4,512,256]{2,1,0:T(8,128)(2,1)S(1)}, u32[]{:S(2)}, u32[]{:S(2)}) %collective-permute-start) | collective-permute-done | bytes 1048608 | tf_op jit(solution)/shard_map/ppermute | solution.py:533
  59.4 3.0 %add_convert_fusion = bf16[4,512,256]{2,1,0:T(8,128)(2,1)} fusion(f32[4,512,256]{2,1,0:T(8,128)} %get-tuple-element.21, bf16[4,512,256]{2,1,0:T(8,128)(2,1)S(1)} %collective-permute-done), kind=kLoop, calls=%fused_computation.1 | loop fusion | flops 1572864 | bytes 4194304 | tf_op jit(solution)/shard_map/convert_element_type | solution.py:554
  62.4 7.1 %all-to-all-start.2 = ((bf16[8,256,256]{2,1,0:T(8,128)(2,1)}), bf16[8,256,256]{2,1,0:T(8,128)(2,1)S(1)}, u32[]{:S(2)}, u32[]{:S(2)}) async-start(bf16[8,256,256]{2,1,0:T(8,128)(2,1)} %bitcast.1), calls=%async_computation.2 | async-start | bytes 2097152 | tf_op jit(solution)/shard_map/all_to_all | solution.py:541
  69.4 15.8 %all-to-all-done.2 = bf16[8,256,256]{2,1,0:T(8,128)(2,1)S(1)} async-done(((bf16[8,256,256]{2,1,0:T(8,128)(2,1)}), bf16[8,256,256]{2,1,0:T(8,128)(2,1)S(1)}, u32[]{:S(2)}, u32[]{:S(2)}) %all-to-all-start.2) | async-done | bytes 1048608 | tf_op jit(solution)/shard_map/all_to_all | solution.py:541
  85.2 0.1 convert_reduce_fusion
  85.3 0.9 subtract_convert_fusion
  86.3 0.1 broadcast_in_dim.2
  86.4 19.2 %all_to_all.31 = bf16[8,256,256]{2,1,0:T(8,128)(2,1)S(1)} all-to-all(bf16[8,256,256]{2,1,0:T(8,128)(2,1)S(1)} %broadcast_in_dim.2), channel_id=1, replica_groups={{0,2,4,6,8,10,12,14},{1,3,5,7,9,11,13,15},{16,18,20,22,24,26,28,30},{17..., dimensions={0} | all-to-all | bytes 2097152 | tf_op jit(solution)/shard_map/all_to_all | solution.py:541
  105.5 0.0 copy-start
  105.5 2.4 %collective-permute-start.1 = (bf16[4,512,256]{2,1,0:T(8,128)(2,1)S(1)}, bf16[4,512,256]{2,1,0:T(8,128)(2,1)S(1)}, u32[]{:S(2)}, u32[]{:S(2)}) collective-permute-start(bf16[4,512,256]{2,1,0:T(8,128)(2,1)S(1)} %bitcast.4), channel_id=1, source_target_pairs={{0,1},{1,0},{2,3},{3,2},{4,5},{5,4},{6,7},{7,6},{8,9},{9,8},{10,11... | collective-permute-start | bytes 3145736 | tf_op jit(solution)/shard_map/ppermute | solution.py:533
  108.0 2.3 %collective-permute-done.1.other.refs_2_ = bf16[4,512,256]{2,1,0:T(8,128)(2,1)S(1)} collective-permute-done((bf16[4,512,256]{2,1,0:T(8,128)(2,1)S(1)}, bf16[4,512,256]{2,1,0:T(8,128)(2,1)S(1)}, u32[]{:S(2)}, u32[]{:S(2)}) %collective-permute-start.1) | collective-permute-done | bytes 1048608 | tf_op jit(solution)/shard_map/ppermute | solution.py:533
  110.3 0.0 copy-done
  110.3 0.0 copy-start.1
  110.3 1.0 copy-done.1
  111.2 11.5 %grad_act.1 = bf16[8,256,128]{2,1,0:T(8,128)(2,1)} custom-call(s32[8,256,128]{2,1,0:T(8,128)} %get-tuple-element.16.columns, bf16[4,512,256]{2,1,0:T(8,128)(2,1)} %bitcast.5, bf16[4,512,256]{2,1,0:T(8,128)(2,1)} %copy-done.1, bf16[36,512,256]{2,1,0:T(8,128)(2,1)} %decoder.3), custom_call_target="tpu_custom_call" | custom-call | tf_op jit(solution)/shard_map/grad_act/pallas_call | solution.py:395
  122.8 3.5 %all-to-all-start.4 = ((bf16[8,256,128]{2,1,0:T(8,128)(2,1)}), bf16[8,256,128]{2,1,0:T(8,128)(2,1)S(1)}, u32[]{:S(2)}, u32[]{:S(2)}) async-start(bf16[8,256,128]{2,1,0:T(8,128)(2,1)} %grad_act.1), calls=%async_computation.4 | async-start | bytes 1048576 | tf_op jit(solution)/shard_map/all_to_all | solution.py:537
  126.3 6.6 %grad_decoder_0.1.refs_3_ = bf16[36,512,256]{2,1,0:T(8,128)(2,1)} custom-call(bf16[8,512,512]{2,1,0:T(8,128)(2,1)} %get-tuple-element.23.refs_0_, bf16[4,512,256]{2,1,0:T(8,128)(2,1)} %bitcast.6, bf16[4,512,256]{2,1,0:T(8,128)(2,1)} %copy-done.1), custom_call_target="tpu_custom_call" | custom-call | flops 2818572288 | bytes 5505024 | tf_op jit(solution)/shard_map/grad_decoder_0/pallas_call | solution.py:450
  132.8 3.6 %all-to-all-done.4.parts = bf16[8,256,128]{2,1,0:T(8,128)(2,1)S(1)} async-done(((bf16[8,256,128]{2,1,0:T(8,128)(2,1)}), bf16[8,256,128]{2,1,0:T(8,128)(2,1)S(1)}, u32[]{:S(2)}, u32[]{:S(2)}) %all-to-all-start.4) | async-done | bytes 524320 | tf_op jit(solution)/shard_map/all_to_all | solution.py:537
  136.5 0.0 copy-start.3
  136.5 0.8 copy-done.3
  137.3 2.0 %settle.3 = bf16[8,256,128]{2,1,0:T(8,128)(2,1)} custom-call(bf16[8,256,128]{2,1,0:T(8,128)(2,1)} %copy-done.3, s32[256,128]{1,0:T(8,128)} %get-tuple-element.19.order), custom_call_target="tpu_custom_call" | custom-call | tf_op jit(solution)/shard_map/settle/pallas_call | solution.py:241
  139.4 3.7 %all-to-all-start.5 = ((bf16[8,256,128]{2,1,0:T(8,128)(2,1)}), bf16[8,256,128]{2,1,0:T(8,128)(2,1)S(1)}, u32[]{:S(2)}, u32[]{:S(2)}) async-start(bf16[8,256,128]{2,1,0:T(8,128)(2,1)} %settle.3), calls=%async_computation.5 | async-start | bytes 1048576 | tf_op jit(solution)/shard_map/all_to_all | solution.py:537
  143.1 3.5 %turn.1.turned_in = bf16[8,256,512]{2,1,0:T(8,128)(2,1)} custom-call(bf16[8,512,256]{2,1,0:T(8,128)(2,1)} %acts.2), custom_call_target="tpu_custom_call" | custom-call | flops 1000000000 | bytes 4194304 | tf_op jit(solution)/shard_map/turn/pallas_call | solution.py:220
  146.6 6.0 %grad_decoder_3.1 = bf16[36,512,256]{2,1,0:T(8,128)(2,1)} custom-call(bf16[8,512,512]{2,1,0:T(8,128)(2,1)} %get-tuple-element.23.refs_0_, bf16[4,512,256]{2,1,0:T(8,128)(2,1)} %bitcast.7, bf16[4,512,256]{2,1,0:T(8,128)(2,1)} %copy-done.1, bf16[36,512,256]{2,1,0:T(8,128)(2,1)} %grad_decoder_0.1.refs_3_), custom_call_target="tpu_custom_call", output_to_operand_aliasing={{}: (3, {})} | custom-call | flops 2013265920 | bytes 3932160 | tf_op jit(solution)/shard_map/grad_decoder_3/pallas_call | solution.py:450
  152.6 0.5 all-to-all-done.5.slots
  153.0 0.0 copy-start.4
  153.0 0.8 copy-done.4
  153.9 10.6 %grad_encoder.1 = (bf16[8,256,512]{2,1,0:T(8,128)(2,1)}, f32[8,512]{1,0:T(8,128)}) custom-call(s32[8,512,512]{2,1,0:T(8,128)} %get-tuple-element.17.ranks_in, bf16[8,256,128]{2,1,0:T(8,128)(2,1)} %copy-done.4, bf16[8,256,512]{2,1,0:T(8,128)(2,1)} %turn.1.turned_in), custom_call_target="tpu_custom_call" | custom-call | tf_op jit(solution)/shard_map/grad_encoder/pallas_call | solution.py:507
Async XLA Ops:
  8.6 17.2 %all-to-all-start = ((bf16[8,256,128]{2,1,0:T(8,128)(2,1)}), bf16[8,256,128]{2,1,0:T(8,128)(2,1)S(1)}, u32[]{:S(2)}, u32[]{:S(2)}) async-start(bf16[8,256,128]{2,1,0:T(8,128)(2,1)} %get-tuple-element.18), calls=%async_computation | async-start | bytes 1048576 | tf_op jit(solution)/shard_map/all_to_all | solution.py:537
  25.9 0.8 copy-start.2
  54.8 4.6 %collective-permute-start = (bf16[4,512,256]{2,1,0:T(8,128)(2,1)}, bf16[4,512,256]{2,1,0:T(8,128)(2,1)S(1)}, u32[]{:S(2)}, u32[]{:S(2)}) collective-permute-start(bf16[4,512,256]{2,1,0:T(8,128)(2,1)} %get-tuple-element.22), channel_id=1, source_target_pairs={{0,1},{1,0},{2,3},{3,2},{4,5},{5,4},{6,7},{7,6},{8,9},{9,8},{10,11... | collective-permute-start | bytes 3145736 | tf_op jit(solution)/shard_map/ppermute | solution.py:533
  62.4 22.8 %all-to-all-start.2 = ((bf16[8,256,256]{2,1,0:T(8,128)(2,1)}), bf16[8,256,256]{2,1,0:T(8,128)(2,1)S(1)}, u32[]{:S(2)}, u32[]{:S(2)}) async-start(bf16[8,256,256]{2,1,0:T(8,128)(2,1)} %bitcast.1), calls=%async_computation.2 | async-start | bytes 2097152 | tf_op jit(solution)/shard_map/all_to_all | solution.py:541
  105.5 4.7 %copy-start = (bf16[8,256,256]{2,1,0:T(8,128)(2,1)}, bf16[8,256,256]{2,1,0:T(8,128)(2,1)S(1)}, u32[]{:S(2)}) copy-start(bf16[8,256,256]{2,1,0:T(8,128)(2,1)S(1)} %all_to_all.31) | copy-start | bytes 3145732
  105.5 4.7 %collective-permute-start.1 = (bf16[4,512,256]{2,1,0:T(8,128)(2,1)S(1)}, bf16[4,512,256]{2,1,0:T(8,128)(2,1)S(1)}, u32[]{:S(2)}, u32[]{:S(2)}) collective-permute-start(bf16[4,512,256]{2,1,0:T(8,128)(2,1)S(1)} %bitcast.4), channel_id=1, source_target_pairs={{0,1},{1,0},{2,3},{3,2},{4,5},{5,4},{6,7},{7,6},{8,9},{9,8},{10,11... | collective-permute-start | bytes 3145736 | tf_op jit(solution)/shard_map/ppermute | solution.py:533
  110.3 1.0 copy-start.1
  122.8 13.7 %all-to-all-start.4 = ((bf16[8,256,128]{2,1,0:T(8,128)(2,1)}), bf16[8,256,128]{2,1,0:T(8,128)(2,1)S(1)}, u32[]{:S(2)}, u32[]{:S(2)}) async-start(bf16[8,256,128]{2,1,0:T(8,128)(2,1)} %grad_act.1), calls=%async_computation.4 | async-start | bytes 1048576 | tf_op jit(solution)/shard_map/all_to_all | solution.py:537
  136.5 0.8 copy-start.3
  139.4 13.7 %all-to-all-start.5 = ((bf16[8,256,128]{2,1,0:T(8,128)(2,1)}), bf16[8,256,128]{2,1,0:T(8,128)(2,1)S(1)}, u32[]{:S(2)}, u32[]{:S(2)}) async-start(bf16[8,256,128]{2,1,0:T(8,128)(2,1)} %settle.3), calls=%async_computation.5 | async-start | bytes 1048576 | tf_op jit(solution)/shard_map/all_to_all | solution.py:537
  153.0 0.8 copy-start.4
